TPU v7x, 32 devices: a 4x4x1 block of a 4x4x8 slice. The times are simulated.
32 devices in a mesh: batch: 1 (over z), seq: 32 (over y, x, core).
Axes of the slice: x: 4, y: 4, z: 1, core: 2. Of those that a mesh axis runs over, the one named last changes fastest.
The devices are a block of a 4x4x8 slice.
Arguments:
- hidden: bfloat16 [32, 4, 7168], P('batch')
- cache_lens: int32 [32], P('batch')
- c_kv: bfloat16 [32, 32768, 512], P('batch', 'seq')
- k_r: bfloat16 [32, 32768, 64], P('batch', 'seq')
- w_uq: bfloat16 [7168, 64, 128], P(None, 'seq')
- w_qr: bfloat16 [7168, 64, 64], P(None, 'seq')
- w_uk: bfloat16 [64, 128, 512], P('seq')
- w_uv: bfloat16 [64, 512, 128], P('seq')
- w_o: bfloat16 [64, 128, 7168], P('seq')
Outputs:
- output: bfloat16 [32, 4, 7168], P('batch')
All inputs are finite; a program needn't handle non-finite values.
Results may differ from a plain program's by a relative error of at most 0.00646674.
Values are sent between devices in bfloat16 or wider.
A program may use at most 768 MiB of HBM per device.

v0:
```python
import jax
import jax.numpy as jnp
from jax import lax
from jax.sharding import PartitionSpec as P

MASK_FILL = -1e30


def solution(mesh):
    def local_step(hidden, cache_lens, c_kv, k_r, w_uq, w_qr, w_uk, w_uv, w_o):
        score_scale = (w_uq.shape[2] + w_qr.shape[2]) ** -0.5
        q_nope = jnp.einsum("cre,eil->cril", hidden, w_uq, preferred_element_type=jnp.float32).astype(jnp.bfloat16)
        q_rope = jnp.einsum("cre,eis->cris", hidden, w_qr, preferred_element_type=jnp.float32).astype(jnp.bfloat16)
        q_lat = jnp.einsum("bqhk,hkc->bqhc", q_nope, w_uk, preferred_element_type=jnp.float32).astype(jnp.bfloat16)
        lat_all = lax.all_gather(q_lat, "seq", axis=2, tiled=True)
        rope_all = lax.all_gather(q_rope, "seq", axis=2, tiled=True)
        local_len = c_kv.shape[1]
        positions = lax.axis_index("seq") * local_len + jnp.arange(local_len)
        limits = cache_lens[:, None] + jnp.arange(hidden.shape[1])[None, :]
        visible = positions[None, None, None, :] <= limits[:, :, None, None]
        scores = (jnp.einsum("bqhc,btc->bqht", lat_all, c_kv, preferred_element_type=jnp.float32)
                  + jnp.einsum("bqhr,btr->bqht", rope_all, k_r, preferred_element_type=jnp.float32)) * score_scale
        scores = jnp.where(visible, scores, MASK_FILL)
        local_max = jnp.max(scores, axis=-1)
        weights = jnp.exp(scores - local_max[..., None])
        local_sum = jnp.sum(weights, axis=-1)
        o_part = jnp.einsum("bqht,btc->bqhc", weights.astype(jnp.bfloat16), c_kv, preferred_element_type=jnp.float32)
        global_max = lax.pmax(local_max, "seq")
        rescale = jnp.exp(local_max - global_max)
        o_sum = lax.psum_scatter(o_part * rescale[..., None], "seq", scatter_dimension=2, tiled=True)
        l_sum = lax.psum_scatter(local_sum * rescale, "seq", scatter_dimension=2, tiled=True)
        o_lat = (o_sum / l_sum[..., None]).astype(jnp.bfloat16)
        o_val = jnp.einsum("bqhc,hcv->bqhv", o_lat, w_uv, preferred_element_type=jnp.float32).astype(jnp.bfloat16)
        y_part = jnp.einsum("criw,iwe->cre", o_val, w_o, preferred_element_type=jnp.float32)
        y_sum = lax.psum(y_part, "seq")
        return (hidden.astype(jnp.float32) + y_sum).astype(jnp.bfloat16)

    specs_in = (P("batch", None, None), P("batch"), P("batch", "seq", None), P("batch", "seq", None),
                P(None, "seq", None), P(None, "seq", None), P("seq", None, None), P("seq", None, None),
                P("seq", None, None))
    return jax.shard_map(local_step, mesh=mesh, in_specs=specs_in, out_specs=P("batch", None, None), check_vma=False)
```

profile of v0, /device:TPU:97, one launch (start us, length us, event | category | flops | bytes accessed | tf_op | source)
XLA Modules:
  0.0 456.4 jit_solution(10585912739058204584)
XLA Ops:
  6.6 0.0 all-gather.3.cloned.1.call-start
  6.6 3.6 fusion.31
  10.2 0.0 copy-start.4
  10.2 0.9 fusion.25
  11.1 0.1 all-gather.3.cloned.1.call-update
  11.2 0.1 all-gather.5.cloned.1.call-start
  11.2 0.0 copy-done
  11.2 3.2 fusion.26
  14.5 0.1 all-gather.5.cloned.1.call-update
  14.5 0.1 reduce-scatter.2.cloned.1.call-start
  14.6 0.0 copy-done.4
  14.6 0.1 iota_add_fusion
  14.7 0.2 broadcast_compare_fusion
  14.9 48.0 %all-gather.3.cloned.1.call-done = bf16[32,4,64,512]{3,0,1,2:T(8,128)(2,1)} async-done(((bf16[32,4,2,512]{3,0,1,2:T(8,128)(2,1)}), bf16[32,4,64,512]{3,0,1,2:T(8,128)(2,1)}) %all-gather.3.cloned.1.call-update) | async-done | bytes 8388624 | tf_op jit(solution)/shard_map/all_gather | solution.py:15
  62.9 35.4 %fusion.2 = f32[32,4,64,1024]{3,2,1,0:T(8,128)} fusion(bf16[32,1024,512]{2,1,0:T(8,128)(2,1)} %param.11, bf16[32,4,64,512]{3,0,1,2:T(8,128)(2,1)} %all-gather.3.cloned.1.call-done), kind=kOutput, calls=%fused_computation.2 | convolution fusion | flops 8589934592 | bytes 75497472 | tf_op jit(solution)/shard_map/bqhc,btc->bqht/dot_general | solution.py:21
  98.3 4.6 all-gather.5.cloned.1.call-done
  102.9 24.7 %fusion.44 = (f32[32,4,64]{2,1,0:T(4,128)S(1)}, f32[32,4,64,1024]{3,2,1,0:T(8,128)}) fusion(f32[32,4,64,1024]{3,2,1,0:T(8,128)} %fusion.2, bf16[32,1024,64]{1,2,0:T(8,128)(2,1)} %param.12, bf16[32,4,64,64]{3,0,1,2:T(8,128)(2,1)} %all-gather.5.cloned.1.call-done, pred[32,4,1024]{2,1,0:T(4,128)(4,1)S(1)} %broadcast_compare_fusion), kind=kOutput, calls=%fused_computation.41 | convolution fusion | flops 1107288064 | bytes 72515584 | tf_op jit(solution)/shard_map/bqhr,btr->bqht/dot_general | solution.py:22
  127.5 44.8 %pmax.7 = f32[32,4,64]{2,1,0:T(4,128)S(1)} all-reduce(f32[32,4,64]{2,1,0:T(4,128)S(1)} %get-tuple-element.7), channel_id=1, replica_groups=mesh['batch'=1,'seq'=32] {'seq'}, use_global_device_ids=true, to_apply=%region_1.2 | all-reduce | flops 8192 | bytes 65536 | tf_op jit(solution)/shard_map/pmax | solution.py:28
  172.3 13.7 %fusion.4 = f32[32,4,64]{2,1,0:T(4,128)S(1)} fusion(f32[32,4,64,1024]{3,2,1,0:T(8,128)} %get-tuple-element.8, f32[32,4,64]{2,1,0:T(4,128)S(1)} %get-tuple-element.7), kind=kLoop, calls=%fused_computation.6 | loop fusion | flops 16769024 | bytes 33619968 | tf_op jit(solution)/shard_map/reduce_sum | solution.py:26
  186.1 29.2 %fusion.8 = f32[32,4,64,512]{3,2,1,0:T(8,128)} fusion(bf16[32,1024,512]{2,1,0:T(8,128)(2,1)} %param.11, f32[32,4,64,1024]{3,2,1,0:T(8,128)} %get-tuple-element.8, f32[32,4,64]{2,1,0:T(4,128)S(1)} %get-tuple-element.7, f32[32,4,64]{2,1,0:T(4,128)S(1)} %bitcast.62), kind=kOutput, calls=%fused_computation.9 | convolution fusion | flops 8610906112 | bytes 83951616 | tf_op jit(solution)/shard_map/bqht,btc->bqhc/dot_general | solution.py:27
  215.2 17.7 %copy.24 = f32[32,4,64,512]{3,0,1,2:T(8,128)} copy(f32[32,4,64,512]{3,2,1,0:T(8,128)} %fusion.8) | data formatting | bytes 33554432 | tf_op jit(solution)/shard_map/mul | solution.py:30
  233.0 0.1 reduce-scatter.2.cloned.1.call-update
  233.0 0.1 all-reduce.3.cloned.1.call-start
  233.1 0.1 copy.25
  233.2 45.1 %all-reduce = f32[32,4,64]{0,1,2:T(4,128)S(1)} all-reduce(f32[32,4,64]{0,1,2:T(4,128)S(1)} %copy.25), channel_id=3, replica_groups=mesh['batch'=1,'seq'=32] {'seq'}, use_global_device_ids=true, to_apply=%region_4.5.clone | all-reduce | flops 8192 | bytes 65536
  278.4 59.1 %reduce-scatter.2.cloned.1.call-done = f32[32,4,2,512]{3,0,1,2:T(8,128)} async-done(((f32[32,4,64,512]{3,0,1,2:T(8,128)}), f32[32,4,2,512]{3,0,1,2:T(8,128)}) %reduce-scatter.2.cloned.1.call-update) | async-done | bytes 524304 | tf_op jit(solution)/shard_map/reduce_scatter | solution.py:30
  337.5 4.9 %convolution_bitcast_fusion = f32[32,4,7168]{2,0,1:T(8,128)} fusion(bf16[2,128,7168]{2,1,0:T(8,128)(2,1)} %param.17, bf16[2,512,128]{2,1,0:T(8,128)(2,1)S(1)} %copy-done.2, f32[32,4,2,512]{3,0,1,2:T(8,128)} %reduce-scatter.2.cloned.1.call-done, f32[32,4,2]{0,1,2:T(4,128)S(1)} %constant_dynamic-slice_fusion), kind=kOutput, calls=%fused_computation.10 | convolution fusion | flops 503611392 | bytes 8127488 | tf_op jit(solution)/shard_map/criw,iwe->cre/dot_general | solution.py:34
  342.4 0.1 all-reduce.3.cloned.1.call-update
  342.4 0.0 copy-start.1
  342.4 101.4 %all-reduce.3.cloned.1.call-done = f32[32,4,7168]{2,0,1:T(8,128)} async-done(((f32[32,4,7168]{2,0,1:T(8,128)}), f32[32,4,7168]{2,0,1:T(8,128)}) %all-reduce.3.cloned.1.call-update) | async-done | bytes 3670032 | tf_op jit(solution)/shard_map/psum | solution.py:35
  443.8 3.3 add_convert_fusion
  447.2 2.6 copy.27
  (9 shorter events, 0.0 us)
Async XLA Ops:
  6.5 4.7 %copy-start = (bf16[7168,2,64]{0,2,1:T(8,128)(2,1)S(1)}, bf16[7168,2,64]{0,2,1:T(8,128)(2,1)}, u32[]{:S(2)}) copy-start(bf16[7168,2,64]{0,2,1:T(8,128)(2,1)} %param.14) | copy-start | bytes 5505028
  6.6 3.6 copy-start.3
  6.6 56.4 %all-gather.3.cloned.1.call-start = ((), (), s32[]{:S(2)}) async-start(), calls=%async_computation.1 | async-start | bytes 8650752 | tf_op jit(solution)/shard_map/all_gather | solution.py:15
  10.2 4.5 copy-start.4
  11.2 91.7 %all-gather.5.cloned.1.call-start = ((), (), s32[]{:S(2)}) async-start(), calls=%async_computation.2 | async-start | bytes 2162688 | tf_op jit(solution)/shard_map/all_gather | solution.py:16
  14.5 322.9 %reduce-scatter.2.cloned.1.call-start = ((), (), s32[]{:S(2)}) async-start(), calls=%async_computation.3 | async-start | bytes 17301504 | tf_op jit(solution)/shard_map/reduce_scatter | solution.py:30
  233.0 104.5 %copy-start.2 = (bf16[2,512,128]{2,1,0:T(8,128)(2,1)S(1)}, bf16[2,512,128]{2,1,0:T(8,128)(2,1)}, u32[]{:S(2)}) copy-start(bf16[2,512,128]{2,1,0:T(8,128)(2,1)} %param.16) | copy-start | bytes 786436
  233.0 210.8 %all-reduce.3.cloned.1.call-start = ((), (), s32[]{:S(2)}) async-start(), calls=%async_computation.4 | async-start | bytes 7340032 | tf_op jit(solution)/shard_map/psum | solution.py:35
  342.4 107.4 %copy-start.1 = (bf16[7168,2,64]{0,2,1:T(8,128)(2,1)S(1)}, bf16[7168,2,64]{0,2,1:T(8,128)(2,1)}, u32[]{:S(2)}) copy-start(bf16[7168,2,64]{0,2,1:T(8,128)(2,1)} %param.14) | copy-start | bytes 5505028
Sparse Core Ops, SparseCore 0:
  11.3 51.5 all-gather.2
  65.0 37.8 all-gather.4
  233.2 104.2 reduce-scatter.1
  342.5 101.2 all-reduce.2
where the time goes:
time: 457 us; the launch traced here: 456 us
  waiting for transfers between devices  213 us (47%)
  matrix products  102 us (22%)
  blocking collectives  90 us (20%)
  local copies, waits for them, and re-layouts  20.5 us (4%)
  other arithmetic  17.3 us (4%)
  between operations  13.3 us (3%)
    psum x1, waiting for transfers between devices, local_step(): y_sum = lax.psum(y_part, 'seq')  101 us
    reduce_scatter x1, waiting for transfers between devices, local_step(): lax.psum_scatter(o_part * rescale[..., None], 'seq', scatter_dimension=2,...  59.1 us
    all_gather x1, waiting for transfers between devices, local_step(): lat_all = lax.all_gather(q_lat, 'seq', axis=2, tiled=True)  48 us
    unnamed x1, blocking collectives  45.1 us
    pmax x1, blocking collectives, local_step(): global_max = lax.pmax(local_max, 'seq')  44.8 us
    dot_general x1, matrix products, local_step(): jnp.einsum('bqhc,btc->bqht', lat_all, c_kv, preferred_element_type=jnp.fl...  35.4 us
    dot_general x1, matrix products, local_step(): jnp.einsum('bqht,btc->bqhc', weights.astype(jnp.bfloat16), c_kv, preferre...  29.2 us
    dot_general x1, matrix products, local_step(): jnp.einsum('bqhr,btr->bqht', rope_all, k_r, preferred_element_type=jnp.fl...  24.7 us
  transfers between devices with their start and end apart: 4, of which 4 were waited for; matrix products, arithmetic and copies ran while one was open for 9% of the time, Pallas kernels for 0%

commit v1 on v0

v1 whole, which is shorter than its diff:
```python
import functools
import math

import jax
import jax.numpy as jnp
from jax import lax
from jax.experimental import pallas as pl
from jax.experimental.pallas import tpu as pltpu
from jax.sharding import PartitionSpec as P

MESH = pl.DeviceIdType.MESH
F32, BF16 = jnp.float32, jnp.bfloat16
FILL = float(jnp.finfo(jnp.float32).min)
CORES = 2
VMEM_BYTES = 67_043_328


class Place:
    def __init__(self, side):
        me = lax.axis_index("seq")
        self.side = side
        self.core = lax.rem(me, CORES)
        chip = me // CORES
        self.x, self.y = lax.rem(chip, side), chip // side
        self.first, self.second = (self.x, self.y), (self.y, self.x)

    def wrap(self, i):
        return lax.rem(i + self.side, self.side)

    def yx(self, plane, f, s):
        return (s, f) if plane == 0 else (f, s)

    def device(self, plane, f, s, core=None):
        y, x = self.yx(plane, f, s)
        return (y * self.side + x) * CORES + (self.core if core is None else core)

    def sibling(self):
        return self.device(0, self.x, self.y, 1 - self.core)

    def along_first(self, plane, step):
        return self.device(plane, self.wrap(self.first[plane] + step), self.second[plane])

    def along_second(self, plane, step):
        return self.device(plane, self.first[plane], self.wrap(self.second[plane] + step))

    def barrier(self):
        barrier = pltpu.get_barrier_semaphore()
        peers = [self.sibling()] + [self.along_first(p, d) for p in range(2) for d in (1, -1)]
        for peer in peers:
            pl.semaphore_signal(barrier, inc=1, device_id={"seq": peer}, device_id_type=MESH)
        pl.semaphore_wait(barrier, len(peers))


def remote(src, dst, send, recv, device):
    return pltpu.make_async_remote_copy(src_ref=src, dst_ref=dst, send_sem=send, recv_sem=recv, device_id={"seq": device},
                                        device_id_type=MESH)


GATHER_MSGS = 12


class Gather:
    def __init__(self, place, plane, view, own, send, recv):
        self.place, self.plane, self.view, self.own, self.send, self.recv = place, plane, view, own, send, recv

    def copy(self, msg, arriving=False):
        pc, p = self.place, self.plane
        f, s, c = pc.first[p], pc.second[p], pc.core
        w = pc.wrap
        sent, got, target = {
            0: ((None, f, s), (None, w(f - 1), s), pc.along_first(p, 1)),
            1: ((None, f, s), (None, w(f + 1), s), pc.along_first(p, -1)),
            2: ((0, w(f - 1), s), (0, w(f - 2), s), pc.along_first(p, 1)),
            3: ((1, w(f + 1), s), (1, w(f + 2), s), pc.along_first(p, -1)),
            4: ((None, None, s), (None, None, w(s - 1)), pc.along_second(p, 1)),
            5: ((None, None, s), (None, None, w(s + 1)), pc.along_second(p, -1)),
            6: ((0, None, w(s - 1)), (0, None, w(s - 2)), pc.along_second(p, 1)),
            7: ((1, None, w(s + 1)), (1, None, w(s + 2)), pc.along_second(p, -1)),
            8: ((None, None, s),) * 2 + (pc.sibling(),),
            9: ((None, None, w(s - 1)),) * 2 + (pc.sibling(),),
            10: ((None, None, w(s + 1)),) * 2 + (pc.sibling(),),
            11: ((None, None, w(s + 2)),) * 2 + (pc.sibling(),),
        }[msg]
        if arriving:
            dst = self.view(1 - c if msg >= 8 else c, *got)
            src = dst
        else:
            dst = self.view(c, *sent)
            src = self.own if msg in (0, 1) else dst
        return remote(src, dst, self.send(msg), self.recv(msg), target)

    def start(self, *msgs):
        for msg in msgs:
            self.copy(msg).start()

    def wait(self, *msgs):
        for msg in msgs:
            self.copy(msg, arriving=True).wait_recv()

    def step(self, i):
        if i == 1:
            self.start(0, 1)
        elif i == 2:
            self.wait(0)
            self.start(2)
            self.wait(1)
            self.start(3)
        elif i == 3:
            self.wait(2, 3)
            self.start(4, 5, 8)
        elif i == 4:
            self.wait(4)
            self.start(6, 9)
            self.wait(5)
            self.start(7, 10)
        elif i == 5:
            self.wait(6, 7)
            self.start(11)
        elif i == 6:
            self.wait(8, 9, 10, 11)

    def drain(self):
        for msg in range(GATHER_MSGS):
            self.copy(msg).wait_send()


SCATTER_MSGS = 8


class Scatter:
    def __init__(self, place, plane, view, landing, merge, extra, send, recv):
        self.place, self.plane, self.view, self.landing = place, plane, view, landing
        self.merge, self.extra, self.send, self.recv = merge, extra, send, recv

    def plan(self, msg):
        pc, p = self.place, self.plane
        f, s = pc.first[p], pc.second[p]
        w = pc.wrap
        return {
            0: ((0, w(f + 2), None), pc.along_first(p, 1), (0, w(f + 1), None)),
            1: ((1, w(f + 2), None), pc.along_first(p, -1), (1, w(f - 1), None)),
            2: ((None, w(f + 1), None), pc.along_first(p, 1), (None, f, None)),
            3: ((None, w(f - 1), None), pc.along_first(p, -1), (None, f, None)),
            4: ((0, f, w(s + 2)), pc.along_second(p, 1), (0, f, w(s + 1))),
            5: ((1, f, w(s + 2)), pc.along_second(p, -1), (1, f, w(s - 1))),
            6: ((None, f, w(s + 1)), pc.along_second(p, 1), (None, f, s)),
            7: ((None, f, w(s - 1)), pc.along_second(p, -1), (None, f, s)),
        }[msg]

    def copies(self, msg, arriving=False):
        sent, target, _ = self.plan(msg)
        dst = self.landing(msg)
        out = [remote(dst if arriving else self.view(*sent), dst, self.send(msg), self.recv(msg), target)]
        extra = self.extra(msg)
        if extra is not None:
            src, dst = extra
            i = msg + SCATTER_MSGS
            out.append(remote(dst if arriving else src, dst, self.send(i), self.recv(i), target))
        return out

    def start(self, *msgs):
        for msg in msgs:
            for copy in self.copies(msg):
                copy.start()

    def take(self, msg):
        for copy in self.copies(msg, arriving=True):
            copy.wait_recv()
        self.merge(*self.plan(msg)[2], msg)

    def drain(self):
        for msg in range(SCATTER_MSGS):
            for copy in self.copies(msg):
                copy.wait_send()


def attention_kernel(cfg, lens_ref, q_ref, ckv_ref, krt_ref, o_ref, qall, obuf, cbuf, kbuf, stat, xt, tcur, tsend, tland, tpair,
                     factor, pair_land, far1, near1, far2, near2, gsend, grecv, ssend, srecv, psend, precv, csem, ksem):
    side, chunk, q_len, scale = cfg
    place = Place(side)
    core = place.core
    batch, lat = ckv_ref.shape[0], ckv_ref.shape[2]
    rope, local_len = krt_ref.shape[1], krt_ref.shape[2]
    block = q_ref.shape[1]
    rows = CORES * side * side * block
    lanes = side * side * block
    pairs = chunk // 2
    n_chunks = batch // chunk
    part = chunk // 2
    half = part // 2
    n_pairs = batch // 2

    def cache_copies(p, e):
        slot = lax.rem(p, 2) * 2 + e
        row = p * 2 + e
        return (pltpu.make_async_copy(ckv_ref.at[row], cbuf.at[slot], csem.at[slot]),
                pltpu.make_async_copy(krt_ref.at[row], kbuf.at[slot, pl.ds(e * rope, rope)], ksem.at[slot]))

    def fetch(p):
        for e in range(2):
            for copy in cache_copies(p, e):
                copy.start()

    for e in range(2):
        for i in range(2):
            kbuf[i * 2 + e, pl.ds((1 - e) * rope, rope)] = jnp.zeros((rope, local_len), BF16)
    fetch(0)
    fetch(1)

    for p in range(n_pairs):
        qall[p, core, place.y, place.x] = q_ref[p]
    stat[...] = jnp.zeros_like(stat)
    place.barrier()

    def gather(k, plane):
        base = k * pairs + plane * (pairs // 2)

        def view(c, h, f, s):
            if h is None:
                at = pl.ds(base, pairs // 2)
            else:
                at = pl.ds(base + h * (pairs // 4), pairs // 4)
            f = pl.ds(0, side) if f is None else f
            y, x = place.yx(plane, f, s)
            return qall.at[at, c, y, x]

        return Gather(place, plane, view, q_ref.at[pl.ds(base, pairs // 2)], lambda m: gsend.at[k, plane, m],
                      lambda m: grecv.at[k, plane, m])

    def merge_tables(ta, tb):
        m = jnp.maximum(ta, tb)
        ea, eb = jnp.exp2(ta - m), jnp.exp2(tb - m)
        top = lax.broadcasted_iota(jnp.int32, ta.shape, 0) < part
        joined = jnp.where(top, m, ta * pltpu.roll(ea, part, 0) + tb * pltpu.roll(eb, part, 0))
        factor[:, 0:4 * part] = jnp.concatenate([ea, eb], 0).T
        return joined

    def scatter(k, plane):
        base = k * chunk + plane * part

        def span(h):
            return (0, part) if h is None else (h * half, half)

        def view(h, f, s):
            lo, n = span(h)
            s = pl.ds(0, side) if s is None else s
            y, x = place.yx(plane, f, s)
            return obuf.at[pl.ds(base + lo, n), core, y, x]

        def landing(msg):
            return {0: far1, 1: near1, 2: far2, 3: near2}[msg // 2].at[k, plane, msg % 2]

        def extra(msg):
            return tsend.at[k, plane, msg], tland.at[k, plane, msg]

        def merge(h, f, s, msg):
            lo, n = span(h)
            ta = tcur[k, plane]
            joined = merge_tables(ta, tland[k, plane, msg])
            spots = lax.broadcasted_iota(jnp.int32, ta.shape, 1) // block
            ys, xs = spots // side, lax.rem(spots, side)
            fs, ss = (xs, ys) if plane == 0 else (ys, xs)
            mine = fs == f
            if s is not None:
                mine = mine & (ss == s)
            if h is not None:
                b = lax.rem(lax.broadcasted_iota(jnp.int32, ta.shape, 0), part)
                mine = mine & (b >= lo) & (b < lo + n)
            tcur[k, plane] = jnp.where(mine, joined, ta)
            land = landing(msg)
            for j in range(n):
                for i in range(side if s is None else 1):
                    y, x = place.yx(plane, f, i if s is None else s)
                    at = pl.ds(pl.multiple_of((y * side + x) * block, block), block)
                    fa = factor[at, lo + j:lo + j + 1]
                    fb = factor[at, 2 * part + lo + j:2 * part + lo + j + 1]
                    there = land[j, i] if s is None else land[j]
                    obuf[base + lo + j, core, y, x] = obuf[base + lo + j, core, y, x] * fa + there * fb

        return Scatter(place, plane, view, landing, merge, extra, lambda m: ssend.at[k, plane, m],
                       lambda m: srecv.at[k, plane, m])

    def both(make, k, act):
        for plane in range(2):
            act(make(k, plane))

    def snap(sc, k, *msgs):
        for msg in msgs:
            tsend[k, sc.plane, msg] = tcur[k, sc.plane]
        sc.start(*msgs)

    def pair_copies(k, arriving=False):
        there = pair_land.at[k]
        src = there if arriving else obuf.at[pl.ds(k * chunk, chunk), 1 - core]
        tables = tpair.at[k]
        tsrc = tables if arriving else xt.at[k, 1 - core]
        return (remote(src, there, psend.at[k, 0], precv.at[k, 0], place.sibling()),
                remote(tsrc, tables, psend.at[k, 1], precv.at[k, 1], place.sibling()))

    def pair_start(k):
        t = stat[...].T
        for c in range(CORES):
            for plane in range(2):
                xt[k, c, plane] = t[plane * 2 * part:(plane + 1) * 2 * part, c * lanes:(c + 1) * lanes]
        for copy in pair_copies(k):
            copy.start()

    def pair_merge(k):
        for copy in pair_copies(k, arriving=True):
            copy.wait_recv()
        for plane in range(2):
            tcur[k, plane] = merge_tables(xt[k, core, plane], tpair[k, plane])
            base = k * chunk + plane * part

            def spot(i, carry):
                y, x = i // side, lax.rem(i, side)
                at = pl.ds(pl.multiple_of(i * block, block), block)
                for j in range(part):
                    fa, fb = factor[at, j:j + 1], factor[at, 2 * part + j:2 * part + j + 1]
                    obuf[base + j, core, y, x] = (obuf[base + j, core, y, x] * fa
                                                  + pair_land[k, plane * part + j, y, x] * fb)
                return carry

            lax.fori_loop(0, side * side, spot, 0)

    def scatter_step(k, i):
        if i == 0:
            pair_merge(k)
            both(scatter, k, lambda sc: snap(sc, k, 0, 1))
        elif i == 1:
            for msg in (0, 1):
                both(scatter, k, lambda sc: (sc.take(msg), snap(sc, k, msg + 2)))
        elif i == 2:
            both(scatter, k, lambda sc: (sc.take(2), sc.take(3), snap(sc, k, 4, 5)))
        elif i == 3:
            for msg in (4, 5):
                both(scatter, k, lambda sc: (sc.take(msg), snap(sc, k, msg + 2)))
        elif i == 4:
            both(scatter, k, lambda sc: (sc.take(6), sc.take(7)))
            at = pl.ds(pl.multiple_of((place.y * side + place.x) * block, block), block)
            for plane in range(2):
                factor[:, 0:2 * part] = tcur[k, plane].T
                for j in range(part):
                    b = k * chunk + plane * part + j
                    o_ref[b] = (obuf[b, core, place.y, place.x] / factor[at, part + j:part + j + 1]).astype(BF16)

    def attend(p, e, j):
        slot = lax.rem(p, 2) * 2 + e
        for copy in cache_copies(p, e):
            copy.wait()
        b = p * 2 + e
        q = qall[p].reshape(rows, qall.shape[-1])
        cache = cbuf[slot]
        s = lax.dot_general(q[:, e * lat:(e + 1) * lat], cache, (((1,), (1,)), ((), ())), preferred_element_type=F32)
        s += jnp.dot(q[:, 2 * lat:], kbuf[slot], preferred_element_type=F32)
        token = lax.rem(lax.broadcasted_iota(jnp.int32, (rows, 1), 0), q_len)
        first = lax.axis_index("seq") * local_len
        positions = lax.broadcasted_iota(jnp.int32, (1, local_len), 1)
        visible = positions <= (token + (lens_ref[b] - first))
        s = jnp.where(visible, s * (scale * math.log2(math.e)), FILL)
        m = jnp.max(s, axis=1, keepdims=True)
        w = jnp.exp2(s - m)
        l = jnp.sum(w, axis=1, keepdims=True)
        o = jnp.dot(w.astype(BF16), cache, preferred_element_type=F32)
        obuf[b] = o.reshape(CORES, side, side, block, lat)
        r = j * 2 + e
        lane = lax.broadcasted_iota(jnp.int32, stat.shape, 1)
        at = (r // part) * 2 * part + lax.rem(r, part)
        stat[...] = jnp.where(lane == at, m, jnp.where(lane == at + part, l, stat[...]))

    for i in range(1, 7):
        both(gather, 0, lambda g: g.step(i))

    def chunk_body(k, carry):
        more, done = k + 1 < n_chunks, k >= 1

        @pl.when(more)
        def _():
            both(gather, k + 1, lambda g: g.step(1))

        def pair_body(j, carry):
            p = k * pairs + j
            for e in range(2):
                attend(p, e, j)

            @pl.when(p + 2 < n_pairs)
            def _():
                fetch(p + 2)

            for i in range(pairs):
                @pl.when(more & (j == i))
                def _():
                    if i < pairs - 1:
                        both(gather, k + 1, lambda g: g.step(i + 2))
                    else:
                        for n in range(pairs + 1, 7):
                            both(gather, k + 1, lambda g: g.step(n))

                @pl.when(done & (j == i))
                def _():
                    scatter_step(k - 1, i)
                    if i == pairs - 1:
                        scatter_step(k - 1, i + 1)
            return carry

        lax.fori_loop(0, pairs, pair_body, 0)
        pair_start(k)
        return carry

    lax.fori_loop(0, n_chunks, chunk_body, 0)
    for i in range(5):
        scatter_step(n_chunks - 1, i)

    def drain(k, carry):
        both(gather, k, lambda g: g.drain())
        both(scatter, k, lambda sc: sc.drain())
        for copy in pair_copies(k):
            copy.wait_send()
        return carry

    lax.fori_loop(0, n_chunks, drain, 0)


def attention(side, lens, q, ckv, krt, q_len, scale, chunk):
    batch, local_len, lat = ckv.shape
    rope = krt.shape[1]
    block = q.shape[1]
    lanes = side * side * block
    n = batch // chunk
    part, half = chunk // 2, chunk // 4
    dma = pltpu.SemaphoreType.DMA
    scratch = [
        pltpu.VMEM((batch // 2, CORES, side, side, block, q.shape[2]), BF16),
        pltpu.VMEM((batch, CORES, side, side, block, lat), F32),
        pltpu.VMEM((4, local_len, lat), BF16),
        pltpu.VMEM((4, 2 * rope, local_len), BF16),
        pltpu.VMEM((CORES * lanes, 128), F32),
        pltpu.VMEM((n, CORES, 2, 2 * part, lanes), F32),
        pltpu.VMEM((n, 2, 2 * part, lanes), F32),
        pltpu.VMEM((n, 2, SCATTER_MSGS, 2 * part, lanes), F32),
        pltpu.VMEM((n, 2, SCATTER_MSGS, 2 * part, lanes), F32),
        pltpu.VMEM((n, 2, 2 * part, lanes), F32),
        pltpu.VMEM((lanes, 128), F32),
        pltpu.VMEM((n, chunk, side, side, block, lat), F32),
        pltpu.VMEM((n, 2, 2, half, side, block, lat), F32),
        pltpu.VMEM((n, 2, 2, part, side, block, lat), F32),
        pltpu.VMEM((n, 2, 2, half, block, lat), F32),
        pltpu.VMEM((n, 2, 2, part, block, lat), F32),
        dma((n, 2, GATHER_MSGS)), dma((n, 2, GATHER_MSGS)),
        dma((n, 2, 2 * SCATTER_MSGS)), dma((n, 2, 2 * SCATTER_MSGS)),
        dma((n, 2)), dma((n, 2)), dma((4,)), dma((4,)),
    ]
    return pl.pallas_call(
        functools.partial(attention_kernel, (side, chunk, q_len, scale)),
        out_shape=jax.ShapeDtypeStruct((batch, block, lat), BF16),
        in_specs=[pl.BlockSpec(memory_space=pltpu.SMEM), pl.BlockSpec(memory_space=pltpu.VMEM),
                  pl.BlockSpec(memory_space=pl.ANY), pl.BlockSpec(memory_space=pl.ANY)],
        out_specs=pl.BlockSpec(memory_space=pltpu.VMEM),
        scratch_shapes=scratch,
        compiler_params=pltpu.CompilerParams(collective_id=0, has_side_effects=True, vmem_limit_bytes=VMEM_BYTES),
        name="attend_rings",
    )(lens, q, ckv, krt)


def output_kernel(side, ol_ref, wuv_ref, wo_ref, hid_ref, out_ref, y_buf, wo_buf, hid_buf, pair_land, far1, near1, far2, near2,
                  ssend, srecv, gsend, grecv, psend, precv, lsem):
    place = Place(side)
    core = place.core
    heads, _, value = wuv_ref.shape
    rb, width = y_buf.shape[2], y_buf.shape[3]
    mine = width // CORES
    part, half = mine // 2, mine // 4
    tiles = 4
    tile = mine // tiles
    n_rows = ol_ref.shape[0]
    tokens = hid_ref.shape[1]
    owned = rb // tokens

    wo_copy = pltpu.make_async_copy(wo_ref, wo_buf, lsem.at[0])
    wo_copy.start()
    col0 = pl.multiple_of(core * mine, 128)
    spot = place.y * side + place.x
    hid_copy = pltpu.make_async_copy(hid_ref.at[pl.ds(spot * owned, owned), :, pl.ds(col0, mine)], hid_buf, lsem.at[1])
    hid_copy.start()
    place.barrier()

    values = jnp.concatenate([wuv_ref[h] for h in range(heads)], axis=1)
    ov = jnp.dot(ol_ref[...], values, preferred_element_type=F32)
    row_head = lax.rem(lax.broadcasted_iota(jnp.int32, ov.shape, 0) // tokens, heads)
    col_head = lax.broadcasted_iota(jnp.int32, ov.shape, 1) // value
    ov = jnp.where(row_head == col_head, ov, 0.0).astype(BF16)
    shape = (n_rows // heads, n_rows)
    to = lax.broadcasted_iota(jnp.int32, shape, 0)
    frm = lax.broadcasted_iota(jnp.int32, shape, 1)
    same = (to // tokens == frm // (tokens * heads)) & (lax.rem(to, tokens) == lax.rem(frm, tokens))
    ov = jnp.dot(same.astype(F32).astype(BF16), ov, preferred_element_type=F32).astype(BF16)
    wo_copy.wait()

    def columns(c, t):
        return pl.ds(pl.multiple_of(c * mine + t * tile, 128), tile)

    def compute(c, t):
        y = jnp.dot(ov, wo_buf[:, columns(c, t)], preferred_element_type=F32)
        y_buf[:, :, :, columns(c, t)] = y.reshape(side, side, rb, tile)

    def pair_copy(t, arriving=False):
        there = pair_land.at[t]
        src = there if arriving else y_buf.at[:, :, :, columns(1 - core, t)]
        return remote(src, there, psend.at[t], precv.at[t], place.sibling())

    for t in range(tiles):
        compute(1 - core, t)
        pair_copy(t).start()
    for t in range(tiles):
        compute(core, t)
        pair_copy(t, arriving=True).wait_recv()
        y_buf[:, :, :, columns(core, t)] += pair_land[t]

    def cols(plane, h, c):
        lo, n = (0, part) if h is None else (h * half, half)
        return pl.ds(pl.multiple_of(c * mine + plane * part + lo, 128), n)

    def scatter(plane):
        def view(h, f, s):
            s = pl.ds(0, side) if s is None else s
            y, x = place.yx(plane, f, s)
            return y_buf.at[y, x, :, cols(plane, h, core)]

        def landing(msg):
            return {0: far1, 1: near1, 2: far2, 3: near2}[msg // 2].at[plane, msg % 2]

        def merge(h, f, s, msg):
            y, x = place.yx(plane, f, pl.ds(0, side) if s is None else s)
            y_buf[y, x, :, cols(plane, h, core)] += landing(msg)[...]

        return Scatter(place, plane, view, landing, merge, lambda m: None, lambda m: ssend.at[plane, m],
                       lambda m: srecv.at[plane, m])

    scs = [scatter(plane) for plane in range(2)]
    for sc in scs:
        sc.start(0, 1)
    for msg in (0, 1):
        for sc in scs:
            sc.take(msg)
            sc.start(msg + 2)
    for sc in scs:
        sc.take(2)
        sc.take(3)
        sc.start(4, 5)
    for msg in (4, 5):
        for sc in scs:
            sc.take(msg)
            sc.start(msg + 2)
    for sc in scs:
        sc.take(6)
        sc.take(7)
    hid_copy.wait()
    own = pl.ds(col0, mine)
    total = y_buf[place.y, place.x, :, own] + hid_buf[...].astype(F32).reshape(rb, mine)
    out_ref[place.y, place.x, :, own] = total.astype(BF16)

    def gather(plane):
        def view(c, h, f, s):
            f = pl.ds(0, side) if f is None else f
            y, x = place.yx(plane, f, s)
            return out_ref.at[y, x, :, cols(plane, h, c)]

        own = view(core, None, place.first[plane], place.second[plane])
        return Gather(place, plane, view, own, lambda m: gsend.at[plane, m], lambda m: grecv.at[plane, m])

    gs = [gather(plane) for plane in range(2)]
    for i in range(1, 7):
        for g in gs:
            g.step(i)
    for g in gs:
        g.drain()
    for sc in scs:
        sc.drain()
    for t in range(tiles):
        pair_copy(t).wait_send()


def output(side, ol, w_uv, wo, hidden):
    batch, tokens, width = hidden.shape
    rb = batch * tokens // (side * side)
    mine = width // CORES
    dma = pltpu.SemaphoreType.DMA
    return pl.pallas_call(
        functools.partial(output_kernel, side),
        out_shape=jax.ShapeDtypeStruct((side, side, rb, width), BF16),
        in_specs=[pl.BlockSpec(memory_space=pltpu.VMEM), pl.BlockSpec(memory_space=pltpu.VMEM),
                  pl.BlockSpec(memory_space=pl.ANY), pl.BlockSpec(memory_space=pl.ANY)],
        out_specs=pl.BlockSpec(memory_space=pltpu.VMEM),
        scratch_shapes=[
            pltpu.VMEM((side, side, rb, width), F32),
            pltpu.VMEM(wo.shape, BF16),
            pltpu.VMEM((rb // tokens, tokens, mine), BF16),
            pltpu.VMEM((4, side, side, rb, mine // 4), F32),
            pltpu.VMEM((2, 2, side, rb, mine // 4), F32),
            pltpu.VMEM((2, 2, side, rb, mine // 2), F32),
            pltpu.VMEM((2, 2, rb, mine // 4), F32),
            pltpu.VMEM((2, 2, rb, mine // 2), F32),
            dma((2, SCATTER_MSGS)), dma((2, SCATTER_MSGS)), dma((2, GATHER_MSGS)), dma((2, GATHER_MSGS)),
            dma((4,)), dma((4,)), dma((2,)),
        ],
        compiler_params=pltpu.CompilerParams(collective_id=1, has_side_effects=True, vmem_limit_bytes=VMEM_BYTES),
        name="project_rings",
    )(ol, w_uv, wo, hidden)


def solution(mesh):
    side = math.isqrt(mesh.shape["seq"] // CORES)

    def local_step(hidden, cache_lens, c_kv, k_r, w_uq, w_qr, w_uk, w_uv, w_o):
        batch, tokens, width = hidden.shape
        heads, lat = w_uk.shape[0], w_uk.shape[2]
        rope = w_qr.shape[2]
        block = heads * tokens
        scale = (w_uq.shape[2] + rope) ** -0.5
        q_nope = jnp.einsum("cre,eil->cril", hidden, w_uq, preferred_element_type=F32).astype(BF16)
        q_rope = jnp.einsum("cre,eis->cris", hidden, w_qr, preferred_element_type=F32).astype(BF16)
        q_lat = jnp.einsum("bqhk,hkc->bqhc", q_nope, w_uk, preferred_element_type=F32).astype(BF16)
        lat_pairs = q_lat.reshape(batch // 2, 2, tokens, heads, lat).transpose(0, 3, 2, 1, 4).reshape(batch // 2, block, 2 * lat)
        rope_pairs = q_rope.reshape(batch // 2, 2, tokens, heads, rope).transpose(0, 3, 2, 1, 4).reshape(batch // 2, block, 2 * rope)
        q = jnp.concatenate([lat_pairs, rope_pairs], axis=2)
        ol = attention(side, cache_lens, q, c_kv, k_r.transpose(0, 2, 1), tokens, scale, batch // 4)
        out = output(side, ol.reshape(batch * block, lat), w_uv, w_o.reshape(-1, width), hidden)
        return out.reshape(batch, tokens, width)

    specs_in = (P("batch", None, None), P("batch"), P("batch", "seq", None), P("batch", "seq", None),
                P(None, "seq", None), P(None, "seq", None), P("seq", None, None), P("seq", None, None),
                P("seq", None, None))
    return jax.shard_map(local_step, mesh=mesh, in_specs=specs_in, out_specs=P("batch", None, None), check_vma=False)
```

time: 457 us -> 225 us (0.49)
  waiting for transfers between devices: 213 us -> 0 us
  Pallas kernels: 0 us -> 212 us
  matrix products: 102 us -> 6.48 us
  blocking collectives: 90 us -> 0 us
  other arithmetic: 17.3 us -> 0.74 us
  local copies, waits for them, and re-layouts: 20.5 us -> 4.72 us
  between operations: 13.3 us -> 0.08 us
    pallas_call x0 -> x2, Pallas kernels: none -> 212 us  [the longest x1 166 us: attention(): pl.pallas_call(functools.partial(attention_kernel, (side, chunk, q_len, s...]
    psum x1 -> x0, waiting for transfers between devices: 101 us -> none  [local_step(): y_sum = lax.psum(y_part, 'seq')]
    dot_general x7 -> x2, matrix products: 102 us -> 6.48 us  [the longest x1 3.31 us: local_step(): jnp.einsum('cre,eis->cris', hidden, w_qr, preferred_element_type=F32)]
    reduce_scatter x1 -> x0, waiting for transfers between devices: 59.1 us -> none  [local_step(): lax.psum_scatter(o_part * rescale[..., None], 'seq', scatter_dimension=2,...]
    all_gather x2 -> x0, waiting for transfers between devices: 52.5 us -> none  [the longest x1 48 us: local_step(): lat_all = lax.all_gather(q_lat, 'seq', axis=2, tiled=True)]
    unnamed x1 -> x0, blocking collectives: 45.1 us -> none
    pmax x1 -> x0, blocking collectives: 44.8 us -> none  [local_step(): global_max = lax.pmax(local_max, 'seq')]
    mul x2 -> x0, local copies, waits for them, and re-layouts: 17.8 us -> none  [the longest x1 17.7 us: local_step(): o_part * rescale[..., None]]
  transfers between devices with their start and end apart: 4 -> 0, of which waited for: 4 -> 0; matrix products, arithmetic and copies ran while one was open for 9% -> 0% of each run, Pallas kernels for 0% -> 0%
where the time goes in v1:
time: 225 us; the launch traced here: 224 us
  Pallas kernels  212 us (94%)
  matrix products  6.48 us (3%)
  local copies, waits for them, and re-layouts  4.72 us (2%)
    pallas_call x1, Pallas kernels, attention(): pl.pallas_call(functools.partial(attention_kernel, (side, chunk, q_len, s...  166 us
    pallas_call x1, Pallas kernels, output(): pl.pallas_call(functools.partial(output_kernel, side), out_shape=jax.Shap...  46.5 us

profile of v1, /device:TPU:97, one launch (start us, length us, event | category | flops | bytes accessed | tf_op | source)
XLA Modules:
  0.0 224.4 jit_solution(18357421699324627654)
XLA Ops:
  0.0 0.0 copy-start
  0.0 0.0 copy-start.1
  0.0 3.3 %fusion.7 = bf16[32,4,2,64]{3,0,2,1:T(8,128)(2,1)S(1)} fusion(bf16[7168,2,64]{0,2,1:T(8,128)(2,1)} %param.14, bf16[32,4,7168,1]{2,1,0,3:T(4,128)(2,1)} %bitcast.33), kind=kOutput, calls=%fused_computation.8 | convolution fusion | flops 234897408 | bytes 3702784 | tf_op jit(solution)/shard_map/cre,eis->cris/dot_general | solution.py:621
  3.4 0.1 reshape.24
  3.5 0.0 copy-done
  3.5 0.0 copy-done.1
  3.5 3.2 %fusion.6 = bf16[32,4,2,512]{3,0,1,2:T(8,128)(2,1)S(1)} fusion(bf16[7168,2,128,1]{2,1,0,3:T(2,128)(2,1)} %bitcast.39, bf16[32,4,7168,1]{2,1,0,3:T(4,128)(2,1)S(1)} %bitcast.34, bf16[2,128,512]{2,1,0:T(8,128)(2,1)S(1)} %copy-done.1), kind=kOutput, calls=%fused_computation.7 | convolution fusion | flops 503480320 | bytes 6029312 | tf_op jit(solution)/shard_map/bqhk,hkc->bqhc/dot_general | solution.py:622
  6.7 0.1 reshape.21
  6.8 0.2 copy.37
  7.0 0.2 reshape.22
  7.2 0.7 pad_maximum_fusion.q_ref
  7.9 165.9 %attend_rings.1 = bf16[32,8,512]{2,1,0:T(8,128)(2,1)} custom-call(s32[32]{0:T(128)} %lens_ref.1, bf16[16,8,1152]{2,1,0:T(8,128)(2,1)} %pad_maximum_fusion.q_ref, bf16[32,1024,512]{2,1,0:T(8,128)(2,1)} %ckv_ref.1, bf16[32,64,1024]{2,1,0:T(8,128)(2,1)} %bitcast.31), custom_call_target="tpu_custom_call" | custom-call | tf_op jit(solution)/shard_map/attend_rings/pallas_call | solution.py:453
  173.9 46.5 %project_rings.1 = bf16[4,4,8,7168]{3,2,1,0:T(8,128)(2,1)} custom-call(bf16[256,512]{1,0:T(8,128)(2,1)} %bitcast.35, bf16[2,512,128]{2,1,0:T(8,128)(2,1)} %wuv_ref.1, bf16[256,7168]{1,0:T(8,128)(2,1)} %bitcast.32, bf16[32,4,7168]{2,1,0:T(4,128)(2,1)} %hid_ref.1), custom_call_target="tpu_custom_call" | custom-call | tf_op jit(solution)/shard_map/project_rings/pallas_call | solution.py:588
  220.4 4.1 %reshape.27 = bf16[32,4,7168]{2,1,0:T(4,128)(2,1)} reshape(bf16[4,4,8,7168]{3,2,1,0:T(8,128)(2,1)} %project_rings.1) | data formatting | bytes 3670016 | tf_op jit(solution)/shard_map/reshape | solution.py:628
  (1 shorter events, 0.0 us)
Async XLA Ops:
  0.0 3.5 %copy-start = (bf16[32,4,7168]{2,1,0:T(4,128)(2,1)S(1)}, bf16[32,4,7168]{2,1,0:T(4,128)(2,1)}, u32[]{:S(2)}) copy-start(bf16[32,4,7168]{2,1,0:T(4,128)(2,1)} %hid_ref.1) | copy-start | bytes 5505028
  0.0 3.5 %copy-start.1 = (bf16[2,128,512]{2,1,0:T(8,128)(2,1)S(1)}, bf16[2,128,512]{2,1,0:T(8,128)(2,1)}, u32[]{:S(2)}) copy-start(bf16[2,128,512]{2,1,0:T(8,128)(2,1)} %param.15) | copy-start | bytes 786436

commit v2 on v1

--- a/solution.py
+++ b/solution.py
@@ -13,6 +13,8 @@
 FILL = float(jnp.finfo(jnp.float32).min)
 CORES = 2
 VMEM_BYTES = 67_043_328
+TOP = 4
+GATHER_SKEW = 2
 
 
 class Place:
@@ -163,9 +165,13 @@
             for copy in self.copies(msg):
                 copy.start()
 
+    def arrive(self, *msgs):
+        for msg in msgs:
+            for copy in self.copies(msg, arriving=True):
+                copy.wait_recv()
+
     def take(self, msg):
-        for copy in self.copies(msg, arriving=True):
-            copy.wait_recv()
+        self.arrive(msg)
         self.merge(*self.plan(msg)[2], msg)
 
     def drain(self):
@@ -176,7 +182,7 @@
 
 def attention_kernel(cfg, lens_ref, q_ref, ckv_ref, krt_ref, o_ref, qall, obuf, cbuf, kbuf, stat, xt, tcur, tsend, tland, tpair,
                      factor, pair_land, far1, near1, far2, near2, gsend, grecv, ssend, srecv, psend, precv, csem, ksem):
-    side, chunk, q_len, scale = cfg
+    side, chunk, gather_pairs, q_len, scale = cfg
     place = Place(side)
     core = place.core
     batch, lat = ckv_ref.shape[0], ckv_ref.shape[2]
@@ -184,11 +190,12 @@
     block = q_ref.shape[1]
     rows = CORES * side * side * block
     lanes = side * side * block
+    n_pairs = batch // 2
+    n_gather = n_pairs // gather_pairs
+    n_chunks = batch // chunk
     pairs = chunk // 2
-    n_chunks = batch // chunk
     part = chunk // 2
     half = part // 2
-    n_pairs = batch // 2
 
     def cache_copies(p, e):
         slot = lax.rem(p, 2) * 2 + e
@@ -213,27 +220,45 @@
     place.barrier()
 
     def gather(k, plane):
-        base = k * pairs + plane * (pairs // 2)
+        base = k * gather_pairs + plane * (gather_pairs // 2)
 
         def view(c, h, f, s):
             if h is None:
-                at = pl.ds(base, pairs // 2)
+                at = pl.ds(base, gather_pairs // 2)
             else:
-                at = pl.ds(base + h * (pairs // 4), pairs // 4)
+                at = pl.ds(base + h * (gather_pairs // 4), gather_pairs // 4)
             f = pl.ds(0, side) if f is None else f
             y, x = place.yx(plane, f, s)
             return qall.at[at, c, y, x]
 
-        return Gather(place, plane, view, q_ref.at[pl.ds(base, pairs // 2)], lambda m: gsend.at[k, plane, m],
+        return Gather(place, plane, view, q_ref.at[pl.ds(base, gather_pairs // 2)], lambda m: gsend.at[k, plane, m],
                       lambda m: grecv.at[k, plane, m])
 
-    def merge_tables(ta, tb):
-        m = jnp.maximum(ta, tb)
-        ea, eb = jnp.exp2(ta - m), jnp.exp2(tb - m)
-        top = lax.broadcasted_iota(jnp.int32, ta.shape, 0) < part
-        joined = jnp.where(top, m, ta * pltpu.roll(ea, part, 0) + tb * pltpu.roll(eb, part, 0))
-        factor[:, 0:4 * part] = jnp.concatenate([ea, eb], 0).T
-        return joined
+    def fold(k, tables, masks):
+        exps = []
+        for plane in range(2):
+            ts = tables[plane]
+            m = functools.reduce(jnp.maximum, ts)
+            es = [jnp.exp2(t - m) for t in ts]
+            top = lax.broadcasted_iota(jnp.int32, m.shape, 0) < TOP
+            sums = functools.reduce(jnp.add, [t * pltpu.roll(e, TOP, 0) for t, e in zip(ts, es)])
+            joined = jnp.where(top, m, sums)
+            tcur[k, plane] = joined if masks is None else jnp.where(masks[plane], joined, ts[0])
+            exps += es
+        factor[:, 0:8 * len(exps)] = jnp.concatenate(exps, 0).T
+
+    def factors(i, y, x, j, n):
+        at = pl.ds(pl.multiple_of((y * side + x) * block, block), block)
+        return [factor[at, 8 * (i * n + t) + j:8 * (i * n + t) + j + 1] for t in range(n)]
+
+    def region(plane, lo, n, f, s):
+        shape = (8, lanes)
+        spots = lax.broadcasted_iota(jnp.int32, shape, 1) // block
+        ys, xs = spots // side, lax.rem(spots, side)
+        fs, ss = (xs, ys) if plane == 0 else (ys, xs)
+        b = lax.rem(lax.broadcasted_iota(jnp.int32, shape, 0), TOP)
+        mine = (fs == f) & (b >= lo) & (b < lo + n)
+        return mine if s is None else mine & (ss == s)
 
     def scatter(k, plane):
         base = k * chunk + plane * part
@@ -253,32 +278,48 @@
         def extra(msg):
             return tsend.at[k, plane, msg], tland.at[k, plane, msg]
 
-        def merge(h, f, s, msg):
-            lo, n = span(h)
+        return Scatter(place, plane, view, landing, None, extra, lambda m: ssend.at[k, plane, m],
+                       lambda m: srecv.at[k, plane, m])
+
+    def merge_far(k, msgs):
+        tables, masks, jobs = [], [], []
+        for plane in range(2):
+            sc = scatter(k, plane)
             ta = tcur[k, plane]
-            joined = merge_tables(ta, tland[k, plane, msg])
-            spots = lax.broadcasted_iota(jnp.int32, ta.shape, 1) // block
-            ys, xs = spots // side, lax.rem(spots, side)
-            fs, ss = (xs, ys) if plane == 0 else (ys, xs)
-            mine = fs == f
-            if s is not None:
-                mine = mine & (ss == s)
-            if h is not None:
-                b = lax.rem(lax.broadcasted_iota(jnp.int32, ta.shape, 0), part)
-                mine = mine & (b >= lo) & (b < lo + n)
-            tcur[k, plane] = jnp.where(mine, joined, ta)
-            land = landing(msg)
+            tb, mask = ta, None
+            for msg in msgs:
+                h, f, s = sc.plan(msg)[2]
+                here = region(plane, h * half, half, f, s)
+                tb = jnp.where(here, tland[k, plane, msg], tb)
+                mask = here if mask is None else mask | here
+                jobs.append((plane, h * half, half, f, s, [sc.landing(msg)]))
+            tables.append([ta, tb])
+            masks.append(mask)
+        fold(k, tables, masks)
+        apply(k, jobs)
+
+    def merge_near(k, msgs):
+        tables, masks, jobs = [], [], []
+        for plane in range(2):
+            sc = scatter(k, plane)
+            _, f, s = sc.plan(msgs[0])[2]
+            tables.append([tcur[k, plane]] + [tland[k, plane, msg] for msg in msgs])
+            masks.append(region(plane, 0, part, f, s))
+            jobs.append((plane, 0, part, f, s, [sc.landing(msg) for msg in msgs]))
+        fold(k, tables, masks)
+        apply(k, jobs)
+
+    def apply(k, jobs):
+        for plane, lo, n, f, s, lands in jobs:
             for j in range(n):
+                b = k * chunk + plane * part + lo + j
                 for i in range(side if s is None else 1):
                     y, x = place.yx(plane, f, i if s is None else s)
-                    at = pl.ds(pl.multiple_of((y * side + x) * block, block), block)
-                    fa = factor[at, lo + j:lo + j + 1]
-                    fb = factor[at, 2 * part + lo + j:2 * part + lo + j + 1]
-                    there = land[j, i] if s is None else land[j]
-                    obuf[base + lo + j, core, y, x] = obuf[base + lo + j, core, y, x] * fa + there * fb
-
-        return Scatter(place, plane, view, landing, merge, extra, lambda m: ssend.at[k, plane, m],
-                       lambda m: srecv.at[k, plane, m])
+                    fs = factors(plane, y, x, lo + j, 1 + len(lands))
+                    total = obuf[b, core, y, x] * fs[0]
+                    for land, fac in zip(lands, fs[1:]):
+                        total += (land[j, i] if s is None else land[j]) * fac
+                    obuf[b, core, y, x] = total
 
     def both(make, k, act):
         for plane in range(2):
@@ -301,50 +342,45 @@
         t = stat[...].T
         for c in range(CORES):
             for plane in range(2):
-                xt[k, c, plane] = t[plane * 2 * part:(plane + 1) * 2 * part, c * lanes:(c + 1) * lanes]
+                xt[k, c, plane] = t[plane * 8:(plane + 1) * 8, c * lanes:(c + 1) * lanes]
         for copy in pair_copies(k):
             copy.start()
 
     def pair_merge(k):
         for copy in pair_copies(k, arriving=True):
             copy.wait_recv()
-        for plane in range(2):
-            tcur[k, plane] = merge_tables(xt[k, core, plane], tpair[k, plane])
-            base = k * chunk + plane * part
-
-            def spot(i, carry):
-                y, x = i // side, lax.rem(i, side)
-                at = pl.ds(pl.multiple_of(i * block, block), block)
+        fold(k, [[xt[k, core, plane], tpair[k, plane]] for plane in range(2)], None)
+
+        def spot(i, carry):
+            y, x = i // side, lax.rem(i, side)
+            for plane in range(2):
                 for j in range(part):
-                    fa, fb = factor[at, j:j + 1], factor[at, 2 * part + j:2 * part + j + 1]
-                    obuf[base + j, core, y, x] = (obuf[base + j, core, y, x] * fa
-                                                  + pair_land[k, plane * part + j, y, x] * fb)
-                return carry
-
-            lax.fori_loop(0, side * side, spot, 0)
+                    b = k * chunk + plane * part + j
+                    fa, fb = factors(plane, y, x, j, 2)
+                    obuf[b, core, y, x] = obuf[b, core, y, x] * fa + pair_land[k, plane * part + j, y, x] * fb
+            return carry
+
+        lax.fori_loop(0, side * side, spot, 0)
 
     def scatter_step(k, i):
         if i == 0:
             pair_merge(k)
             both(scatter, k, lambda sc: snap(sc, k, 0, 1))
-        elif i == 1:
-            for msg in (0, 1):
-                both(scatter, k, lambda sc: (sc.take(msg), snap(sc, k, msg + 2)))
-        elif i == 2:
-            both(scatter, k, lambda sc: (sc.take(2), sc.take(3), snap(sc, k, 4, 5)))
-        elif i == 3:
-            for msg in (4, 5):
-                both(scatter, k, lambda sc: (sc.take(msg), snap(sc, k, msg + 2)))
-        elif i == 4:
-            both(scatter, k, lambda sc: (sc.take(6), sc.take(7)))
-            at = pl.ds(pl.multiple_of((place.y * side + place.x) * block, block), block)
-            for plane in range(2):
-                factor[:, 0:2 * part] = tcur[k, plane].T
-                for j in range(part):
-                    b = k * chunk + plane * part + j
-                    o_ref[b] = (obuf[b, core, place.y, place.x] / factor[at, part + j:part + j + 1]).astype(BF16)
-
-    def attend(p, e, j):
+            return
+        msgs = (2 * i - 2, 2 * i - 1)
+        both(scatter, k, lambda sc: sc.arrive(*msgs))
+        (merge_far if i in (1, 3) else merge_near)(k, msgs)
+        if i < 4:
+            both(scatter, k, lambda sc: snap(sc, k, 2 * i, 2 * i + 1))
+            return
+        factor[:, 0:16] = jnp.concatenate([tcur[k, plane] for plane in range(2)], 0).T
+        for plane in range(2):
+            for j in range(part):
+                b = k * chunk + plane * part + j
+                l = factors(plane, place.y, place.x, TOP + j, 1)[0]
+                o_ref[b] = (obuf[b, core, place.y, place.x] / l).astype(BF16)
+
+    def attend(p, e):
         slot = lax.rem(p, 2) * 2 + e
         for copy in cache_copies(p, e):
             copy.wait()
@@ -363,70 +399,70 @@
         l = jnp.sum(w, axis=1, keepdims=True)
         o = jnp.dot(w.astype(BF16), cache, preferred_element_type=F32)
         obuf[b] = o.reshape(CORES, side, side, block, lat)
-        r = j * 2 + e
+        r = lax.rem(b, chunk)
         lane = lax.broadcasted_iota(jnp.int32, stat.shape, 1)
-        at = (r // part) * 2 * part + lax.rem(r, part)
-        stat[...] = jnp.where(lane == at, m, jnp.where(lane == at + part, l, stat[...]))
-
-    for i in range(1, 7):
-        both(gather, 0, lambda g: g.step(i))
-
-    def chunk_body(k, carry):
-        more, done = k + 1 < n_chunks, k >= 1
-
-        @pl.when(more)
+        at = (r // part) * 8 + lax.rem(r, part)
+        stat[...] = jnp.where(lane == at, m, jnp.where(lane == at + TOP, l, stat[...]))
+
+    last = 6 + GATHER_SKEW * (n_gather - 1)
+    turns = [[(g, turn - GATHER_SKEW * g) for g in range(n_gather) if 1 <= turn - GATHER_SKEW * g <= 6]
+             for turn in range(last + 1)]
+    for turn in turns[:7]:
+        for g, i in turn:
+            both(gather, g, lambda ga: ga.step(i))
+
+    def slot(h, carry):
+        @pl.when(h < n_pairs)
         def _():
-            both(gather, k + 1, lambda g: g.step(1))
-
-        def pair_body(j, carry):
-            p = k * pairs + j
             for e in range(2):
-                attend(p, e, j)
-
-            @pl.when(p + 2 < n_pairs)
+                attend(h, e)
+
+        @pl.when(h + 2 < n_pairs)
+        def _():
+            fetch(h + 2)
+
+        for late, turn in enumerate(turns[7:]):
+            @pl.when(h == late)
             def _():
-                fetch(p + 2)
-
-            for i in range(pairs):
-                @pl.when(more & (j == i))
-                def _():
-                    if i < pairs - 1:
-                        both(gather, k + 1, lambda g: g.step(i + 2))
-                    else:
-                        for n in range(pairs + 1, 7):
-                            both(gather, k + 1, lambda g: g.step(n))
-
-                @pl.when(done & (j == i))
-                def _():
-                    scatter_step(k - 1, i)
-                    if i == pairs - 1:
-                        scatter_step(k - 1, i + 1)
-            return carry
-
-        lax.fori_loop(0, pairs, pair_body, 0)
-        pair_start(k)
+                for g, i in turn:
+                    both(gather, g, lambda ga: ga.step(i))
+
+        for i in reversed(range(5)):
+            k = (h - i) // pairs - 1
+
+            @pl.when((h >= i + pairs) & (lax.rem(h + pairs * 5 - i, pairs) == 0) & (k < n_chunks))
+            def _():
+                scatter_step(k, i)
+
+        @pl.when((h < n_pairs) & (lax.rem(h, pairs) == pairs - 1))
+        def _():
+            pair_start(h // pairs)
+
         return carry
 
-    lax.fori_loop(0, n_chunks, chunk_body, 0)
-    for i in range(5):
-        scatter_step(n_chunks - 1, i)
+    lax.fori_loop(0, n_pairs + 5, slot, 0)
+
+    def drain_gather(k, carry):
+        both(gather, k, lambda g: g.drain())
+        return carry
 
     def drain(k, carry):
-        both(gather, k, lambda g: g.drain())
         both(scatter, k, lambda sc: sc.drain())
         for copy in pair_copies(k):
             copy.wait_send()
         return carry
 
+    lax.fori_loop(0, n_gather, drain_gather, 0)
     lax.fori_loop(0, n_chunks, drain, 0)
 
 
-def attention(side, lens, q, ckv, krt, q_len, scale, chunk):
+def attention(side, lens, q, ckv, krt, q_len, scale, chunk, gather_pairs):
     batch, local_len, lat = ckv.shape
     rope = krt.shape[1]
     block = q.shape[1]
     lanes = side * side * block
     n = batch // chunk
+    n_gather = batch // 2 // gather_pairs
     part, half = chunk // 2, chunk // 4
     dma = pltpu.SemaphoreType.DMA
     scratch = [
@@ -435,23 +471,23 @@
         pltpu.VMEM((4, local_len, lat), BF16),
         pltpu.VMEM((4, 2 * rope, local_len), BF16),
         pltpu.VMEM((CORES * lanes, 128), F32),
-        pltpu.VMEM((n, CORES, 2, 2 * part, lanes), F32),
-        pltpu.VMEM((n, 2, 2 * part, lanes), F32),
-        pltpu.VMEM((n, 2, SCATTER_MSGS, 2 * part, lanes), F32),
-        pltpu.VMEM((n, 2, SCATTER_MSGS, 2 * part, lanes), F32),
-        pltpu.VMEM((n, 2, 2 * part, lanes), F32),
+        pltpu.VMEM((n, CORES, 2, 8, lanes), F32),
+        pltpu.VMEM((n, 2, 8, lanes), F32),
+        pltpu.VMEM((n, 2, SCATTER_MSGS, 8, lanes), F32),
+        pltpu.VMEM((n, 2, SCATTER_MSGS, 8, lanes), F32),
+        pltpu.VMEM((n, 2, 8, lanes), F32),
         pltpu.VMEM((lanes, 128), F32),
         pltpu.VMEM((n, chunk, side, side, block, lat), F32),
         pltpu.VMEM((n, 2, 2, half, side, block, lat), F32),
         pltpu.VMEM((n, 2, 2, part, side, block, lat), F32),
         pltpu.VMEM((n, 2, 2, half, block, lat), F32),
         pltpu.VMEM((n, 2, 2, part, block, lat), F32),
-        dma((n, 2, GATHER_MSGS)), dma((n, 2, GATHER_MSGS)),
+        dma((n_gather, 2, GATHER_MSGS)), dma((n_gather, 2, GATHER_MSGS)),
         dma((n, 2, 2 * SCATTER_MSGS)), dma((n, 2, 2 * SCATTER_MSGS)),
         dma((n, 2)), dma((n, 2)), dma((4,)), dma((4,)),
     ]
     return pl.pallas_call(
-        functools.partial(attention_kernel, (side, chunk, q_len, scale)),
+        functools.partial(attention_kernel, (side, chunk, gather_pairs, q_len, scale)),
         out_shape=jax.ShapeDtypeStruct((batch, block, lat), BF16),
         in_specs=[pl.BlockSpec(memory_space=pltpu.SMEM), pl.BlockSpec(memory_space=pltpu.VMEM),
                   pl.BlockSpec(memory_space=pl.ANY), pl.BlockSpec(memory_space=pl.ANY)],
@@ -623,7 +659,7 @@
         lat_pairs = q_lat.reshape(batch // 2, 2, tokens, heads, lat).transpose(0, 3, 2, 1, 4).reshape(batch // 2, block, 2 * lat)
         rope_pairs = q_rope.reshape(batch // 2, 2, tokens, heads, rope).transpose(0, 3, 2, 1, 4).reshape(batch // 2, block, 2 * rope)
         q = jnp.concatenate([lat_pairs, rope_pairs], axis=2)
-        ol = attention(side, cache_lens, q, c_kv, k_r.transpose(0, 2, 1), tokens, scale, batch // 4)
+        ol = attention(side, cache_lens, q, c_kv, k_r.transpose(0, 2, 1), tokens, scale, batch // 8, batch // 8)
         out = output(side, ol.reshape(batch * block, lat), w_uv, w_o.reshape(-1, width), hidden)
         return out.reshape(batch, tokens, width)
 

time: 225 us -> 212 us (0.942)
  Pallas kernels: 212 us -> 199 us
    pallas_call x1, Pallas kernels: 166 us -> 150 us  [attention(): pl.pallas_call(functools.partial(attention_kernel, (side, chunk, gather_p...]
    pallas_call x1, Pallas kernels: 46.5 us -> 49.7 us  [output(): pl.pallas_call(functools.partial(output_kernel, side), out_shape=jax.Shap...]
where the time goes in v2:
time: 212 us; the launch traced here: 211 us
  Pallas kernels  199 us (94%)
  matrix products  6.48 us (3%)
  local copies, waits for them, and re-layouts  4.72 us (2%)
    pallas_call x1, Pallas kernels, attention(): pl.pallas_call(functools.partial(attention_kernel, (side, chunk, gather_p...  150 us
    pallas_call x1, Pallas kernels, output(): pl.pallas_call(functools.partial(output_kernel, side), out_shape=jax.Shap...  49.7 us

profile of v2, /device:TPU:97, one launch (start us, length us, event | category | flops | bytes accessed | tf_op | source)
XLA Modules:
  0.0 211.5 jit_solution(6239451367805961032)
XLA Ops:
  0.0 0.0 copy-start
  0.0 0.0 copy-start.1
  0.0 3.3 %fusion.7 = bf16[32,4,2,64]{3,0,2,1:T(8,128)(2,1)S(1)} fusion(bf16[7168,2,64]{0,2,1:T(8,128)(2,1)} %param.14, bf16[32,4,7168,1]{2,1,0,3:T(4,128)(2,1)} %bitcast.33), kind=kOutput, calls=%fused_computation.8 | convolution fusion | flops 234897408 | bytes 3702784 | tf_op jit(solution)/shard_map/cre,eis->cris/dot_general | solution.py:657
  3.4 0.1 reshape.24
  3.5 0.0 copy-done
  3.5 0.0 copy-done.1
  3.5 3.2 %fusion.6 = bf16[32,4,2,512]{3,0,1,2:T(8,128)(2,1)S(1)} fusion(bf16[7168,2,128,1]{2,1,0,3:T(2,128)(2,1)} %bitcast.39, bf16[32,4,7168,1]{2,1,0,3:T(4,128)(2,1)S(1)} %bitcast.34, bf16[2,128,512]{2,1,0:T(8,128)(2,1)S(1)} %copy-done.1), kind=kOutput, calls=%fused_computation.7 | convolution fusion | flops 503480320 | bytes 6029312 | tf_op jit(solution)/shard_map/bqhk,hkc->bqhc/dot_general | solution.py:658
  6.7 0.1 reshape.21
  6.8 0.2 copy.37
  7.0 0.2 reshape.22
  7.2 0.7 pad_maximum_fusion.q_ref
  7.9 149.8 %attend_rings.1 = bf16[32,8,512]{2,1,0:T(8,128)(2,1)} custom-call(s32[32]{0:T(128)} %lens_ref.1, bf16[16,8,1152]{2,1,0:T(8,128)(2,1)} %pad_maximum_fusion.q_ref, bf16[32,1024,512]{2,1,0:T(8,128)(2,1)} %ckv_ref.1, bf16[32,64,1024]{2,1,0:T(8,128)(2,1)} %bitcast.31), custom_call_target="tpu_custom_call" | custom-call | tf_op jit(solution)/shard_map/attend_rings/pallas_call | solution.py:489
  157.7 49.7 %project_rings.1 = bf16[4,4,8,7168]{3,2,1,0:T(8,128)(2,1)} custom-call(bf16[256,512]{1,0:T(8,128)(2,1)} %bitcast.35, bf16[2,512,128]{2,1,0:T(8,128)(2,1)} %wuv_ref.1, bf16[256,7168]{1,0:T(8,128)(2,1)} %bitcast.32, bf16[32,4,7168]{2,1,0:T(4,128)(2,1)} %hid_ref.1), custom_call_target="tpu_custom_call" | custom-call | tf_op jit(solution)/shard_map/project_rings/pallas_call | solution.py:624
  207.4 4.1 %reshape.27 = bf16[32,4,7168]{2,1,0:T(4,128)(2,1)} reshape(bf16[4,4,8,7168]{3,2,1,0:T(8,128)(2,1)} %project_rings.1) | data formatting | bytes 3670016 | tf_op jit(solution)/shard_map/reshape | solution.py:664
  (1 shorter events, 0.0 us)
Async XLA Ops:
  0.0 3.5 %copy-start = (bf16[32,4,7168]{2,1,0:T(4,128)(2,1)S(1)}, bf16[32,4,7168]{2,1,0:T(4,128)(2,1)}, u32[]{:S(2)}) copy-start(bf16[32,4,7168]{2,1,0:T(4,128)(2,1)} %hid_ref.1) | copy-start | bytes 5505028
  0.0 3.5 %copy-start.1 = (bf16[2,128,512]{2,1,0:T(8,128)(2,1)S(1)}, bf16[2,128,512]{2,1,0:T(8,128)(2,1)}, u32[]{:S(2)}) copy-start(bf16[2,128,512]{2,1,0:T(8,128)(2,1)} %param.15) | copy-start | bytes 786436

commit v3 on v2

--- a/solution.py
+++ b/solution.py
@@ -14,7 +14,11 @@
 CORES = 2
 VMEM_BYTES = 67_043_328
 TOP = 4
-GATHER_SKEW = 2
+GATHER_TURN = ((1, 2, 3, 4), (2, 3, 5, 6, 7, 8), (4, 5, 7, 9, 11, 12), (6, 7, 10, 12, 14, 16))
+SLOT_TURN = 5
+STEP_SLOT = (0, 3, 6, 8, 10)
+GROUP = 8
+PARTS = 2
 
 
 class Place:
@@ -36,18 +40,15 @@
         y, x = self.yx(plane, f, s)
         return (y * self.side + x) * CORES + (self.core if core is None else core)
 
+    def around(self, i):
+        return self.wrap(i + 1), self.wrap(i - 1), self.wrap(i + 2)
+
     def sibling(self):
         return self.device(0, self.x, self.y, 1 - self.core)
 
-    def along_first(self, plane, step):
-        return self.device(plane, self.wrap(self.first[plane] + step), self.second[plane])
-
-    def along_second(self, plane, step):
-        return self.device(plane, self.first[plane], self.wrap(self.second[plane] + step))
-
     def barrier(self):
         barrier = pltpu.get_barrier_semaphore()
-        peers = [self.sibling()] + [self.along_first(p, d) for p in range(2) for d in (1, -1)]
+        peers = [self.sibling()] + [self.device(p, f, self.second[p]) for p in range(2) for f in self.around(self.first[p])]
         for peer in peers:
             pl.semaphore_signal(barrier, inc=1, device_id={"seq": peer}, device_id_type=MESH)
         pl.semaphore_wait(barrier, len(peers))
@@ -58,37 +59,48 @@
                                         device_id_type=MESH)
 
 
-GATHER_MSGS = 12
+ALL, LOW, HIGH = None, 0, 1
+GATHER_MSGS, TWIN_MSG, RELAYED = 12, 8, (3, 7)
+TWINS = ((8, 9, 10, 11), ())
+RING_STEPS = ((((), (0, 1)),), (((0,), (2,)), ((1,), (3,))), (((2, 3), (4, 5, 8)),), (((4,), (6, 9)), ((5,), (7, 10))),
+              (((6, 7), (11,)),), (TWINS,))
+DIRECT_STEPS = ((((), (0, 1, 2)),), (((0, 1, 2), (4, 5, 6, 8)),), (((4,), (9,)), ((5,), (10,)), ((6,), (11,))), (TWINS,))
 
 
 class Gather:
-    def __init__(self, place, plane, view, own, send, recv):
+    def __init__(self, place, plane, view, own, send, recv, direct=False):
         self.place, self.plane, self.view, self.own, self.send, self.recv = place, plane, view, own, send, recv
+        self.direct = direct
 
     def copy(self, msg, arriving=False):
         pc, p = self.place, self.plane
-        f, s, c = pc.first[p], pc.second[p], pc.core
-        w = pc.wrap
-        sent, got, target = {
-            0: ((None, f, s), (None, w(f - 1), s), pc.along_first(p, 1)),
-            1: ((None, f, s), (None, w(f + 1), s), pc.along_first(p, -1)),
-            2: ((0, w(f - 1), s), (0, w(f - 2), s), pc.along_first(p, 1)),
-            3: ((1, w(f + 1), s), (1, w(f + 2), s), pc.along_first(p, -1)),
-            4: ((None, None, s), (None, None, w(s - 1)), pc.along_second(p, 1)),
-            5: ((None, None, s), (None, None, w(s + 1)), pc.along_second(p, -1)),
-            6: ((0, None, w(s - 1)), (0, None, w(s - 2)), pc.along_second(p, 1)),
-            7: ((1, None, w(s + 1)), (1, None, w(s + 2)), pc.along_second(p, -1)),
-            8: ((None, None, s),) * 2 + (pc.sibling(),),
-            9: ((None, None, w(s - 1)),) * 2 + (pc.sibling(),),
-            10: ((None, None, w(s + 1)),) * 2 + (pc.sibling(),),
-            11: ((None, None, w(s + 2)),) * 2 + (pc.sibling(),),
-        }[msg]
+        f, s, c, twin = pc.first[p], pc.second[p], pc.core, pc.sibling()
+        f_up, f_down, f_far = pc.around(f)
+        s_up, s_down, s_far = pc.around(s)
+        to_f_up, to_f_down, to_f_far = [pc.device(p, i, s) for i in (f_up, f_down, f_far)]
+        to_s_up, to_s_down, to_s_far = [pc.device(p, f, i) for i in (s_up, s_down, s_far)]
+        row = (ALL, ALL, s)
+        plans = [
+            ((ALL, f, s), (ALL, f_down, s), to_f_up),
+            ((ALL, f, s), (ALL, f_up, s), to_f_down),
+            ((LOW, f_down, s), (LOW, f_far, s), to_f_up),
+            ((HIGH, f_up, s), (HIGH, f_far, s), to_f_down),
+            (row, (ALL, ALL, s_down), to_s_up),
+            (row, (ALL, ALL, s_up), to_s_down),
+            ((LOW, ALL, s_down), (LOW, ALL, s_far), to_s_up),
+            ((HIGH, ALL, s_up), (HIGH, ALL, s_far), to_s_down),
+        ]
+        plans += [((ALL, ALL, i), (ALL, ALL, i), twin) for i in (s, s_down, s_up, s_far)]
+        if self.direct:
+            plans[2] = ((ALL, f, s), (ALL, f_far, s), to_f_far)
+            plans[6] = (row, (ALL, ALL, s_far), to_s_far)
+        sent, got, target = plans[msg]
         if arriving:
-            dst = self.view(1 - c if msg >= 8 else c, *got)
+            dst = self.view(1 - c if msg >= TWIN_MSG else c, *got)
             src = dst
         else:
             dst = self.view(c, *sent)
-            src = self.own if msg in (0, 1) else dst
+            src = self.own if sent == (ALL, f, s) else dst
         return remote(src, dst, self.send(msg), self.recv(msg), target)
 
     def start(self, *msgs):
@@ -100,30 +112,14 @@
             self.copy(msg, arriving=True).wait_recv()
 
     def step(self, i):
-        if i == 1:
-            self.start(0, 1)
-        elif i == 2:
-            self.wait(0)
-            self.start(2)
-            self.wait(1)
-            self.start(3)
-        elif i == 3:
-            self.wait(2, 3)
-            self.start(4, 5, 8)
-        elif i == 4:
-            self.wait(4)
-            self.start(6, 9)
-            self.wait(5)
-            self.start(7, 10)
-        elif i == 5:
-            self.wait(6, 7)
-            self.start(11)
-        elif i == 6:
-            self.wait(8, 9, 10, 11)
+        for waits, starts in (DIRECT_STEPS if self.direct else RING_STEPS)[i - 1]:
+            self.wait(*waits)
+            self.start(*starts)
 
     def drain(self):
         for msg in range(GATHER_MSGS):
-            self.copy(msg).wait_send()
+            if not (self.direct and msg in RELAYED):
+                self.copy(msg).wait_send()
 
 
 SCATTER_MSGS = 8
@@ -137,17 +133,20 @@
     def plan(self, msg):
         pc, p = self.place, self.plane
         f, s = pc.first[p], pc.second[p]
-        w = pc.wrap
-        return {
-            0: ((0, w(f + 2), None), pc.along_first(p, 1), (0, w(f + 1), None)),
-            1: ((1, w(f + 2), None), pc.along_first(p, -1), (1, w(f - 1), None)),
-            2: ((None, w(f + 1), None), pc.along_first(p, 1), (None, f, None)),
-            3: ((None, w(f - 1), None), pc.along_first(p, -1), (None, f, None)),
-            4: ((0, f, w(s + 2)), pc.along_second(p, 1), (0, f, w(s + 1))),
-            5: ((1, f, w(s + 2)), pc.along_second(p, -1), (1, f, w(s - 1))),
-            6: ((None, f, w(s + 1)), pc.along_second(p, 1), (None, f, s)),
-            7: ((None, f, w(s - 1)), pc.along_second(p, -1), (None, f, s)),
-        }[msg]
+        f_up, f_down, f_far = pc.around(f)
+        s_up, s_down, s_far = pc.around(s)
+        to_f_up, to_f_down = [pc.device(p, i, s) for i in (f_up, f_down)]
+        to_s_up, to_s_down = [pc.device(p, f, i) for i in (s_up, s_down)]
+        return [
+            ((LOW, f_far, ALL), to_f_up, (LOW, f_up, ALL)),
+            ((HIGH, f_far, ALL), to_f_down, (HIGH, f_down, ALL)),
+            ((ALL, f_up, ALL), to_f_up, (ALL, f, ALL)),
+            ((ALL, f_down, ALL), to_f_down, (ALL, f, ALL)),
+            ((LOW, f, s_far), to_s_up, (LOW, f, s_up)),
+            ((HIGH, f, s_far), to_s_down, (HIGH, f, s_down)),
+            ((ALL, f, s_up), to_s_up, (ALL, f, s)),
+            ((ALL, f, s_down), to_s_down, (ALL, f, s)),
+        ][msg]
 
     def copies(self, msg, arriving=False):
         sent, target, _ = self.plan(msg)
@@ -232,7 +231,7 @@
             return qall.at[at, c, y, x]
 
         return Gather(place, plane, view, q_ref.at[pl.ds(base, gather_pairs // 2)], lambda m: gsend.at[k, plane, m],
-                      lambda m: grecv.at[k, plane, m])
+                      lambda m: grecv.at[k, plane, m], isinstance(k, int) and k == 0)
 
     def fold(k, tables, masks):
         exps = []
@@ -310,16 +309,22 @@
         apply(k, jobs)
 
     def apply(k, jobs):
-        for plane, lo, n, f, s, lands in jobs:
-            for j in range(n):
+        blocks = [(plane, j, i, f, s, lo, lands) for plane, lo, n, f, s, lands in jobs for j in range(n)
+                  for i in range(side if s is None else 1)]
+        facs = []
+        for plane, j, i, f, s, lo, lands in blocks:
+            y, x = place.yx(plane, f, i if s is None else s)
+            facs.append((y, x, factors(plane, y, x, lo + j, 1 + len(lands))))
+        for g in range(0, len(blocks), GROUP):
+            totals = []
+            for (plane, j, i, f, s, lo, lands), (y, x, fs) in zip(blocks[g:g + GROUP], facs[g:g + GROUP]):
                 b = k * chunk + plane * part + lo + j
-                for i in range(side if s is None else 1):
-                    y, x = place.yx(plane, f, i if s is None else s)
-                    fs = factors(plane, y, x, lo + j, 1 + len(lands))
-                    total = obuf[b, core, y, x] * fs[0]
-                    for land, fac in zip(lands, fs[1:]):
-                        total += (land[j, i] if s is None else land[j]) * fac
-                    obuf[b, core, y, x] = total
+                total = obuf[b, core, y, x] * fs[0]
+                for land, fac in zip(lands, fs[1:]):
+                    total += (land[j, i] if s is None else land[j]) * fac
+                totals.append((b, y, x, total))
+            for b, y, x, total in totals:
+                obuf[b, core, y, x] = total
 
     def both(make, k, act):
         for plane in range(2):
@@ -351,16 +356,22 @@
             copy.wait_recv()
         fold(k, [[xt[k, core, plane], tpair[k, plane]] for plane in range(2)], None)
 
-        def spot(i, carry):
-            y, x = i // side, lax.rem(i, side)
-            for plane in range(2):
-                for j in range(part):
+        def spots(t, carry):
+            facs, totals = {}, []
+            spans = [(plane, j, x) for plane in range(2) for j in range(part) for x in range(side)]
+            for plane, j, x in spans:
+                facs[plane, j, x] = factors(plane, t, x, j, 2)
+            for g in range(0, len(spans), GROUP):
+                totals = []
+                for plane, j, x in spans[g:g + GROUP]:
                     b = k * chunk + plane * part + j
-                    fa, fb = factors(plane, y, x, j, 2)
-                    obuf[b, core, y, x] = obuf[b, core, y, x] * fa + pair_land[k, plane * part + j, y, x] * fb
+                    fa, fb = facs[plane, j, x]
+                    totals.append((b, x, obuf[b, core, t, x] * fa + pair_land[k, plane * part + j, t, x] * fb))
+                for b, x, total in totals:
+                    obuf[b, core, t, x] = total
             return carry
 
-        lax.fori_loop(0, side * side, spot, 0)
+        lax.fori_loop(0, side, spots, 0)
 
     def scatter_step(k, i):
         if i == 0:
@@ -404,10 +415,9 @@
         at = (r // part) * 8 + lax.rem(r, part)
         stat[...] = jnp.where(lane == at, m, jnp.where(lane == at + TOP, l, stat[...]))
 
-    last = 6 + GATHER_SKEW * (n_gather - 1)
-    turns = [[(g, turn - GATHER_SKEW * g) for g in range(n_gather) if 1 <= turn - GATHER_SKEW * g <= 6]
-             for turn in range(last + 1)]
-    for turn in turns[:7]:
+    turns = [[(g, i + 1) for g in range(n_gather) for i, at in enumerate(GATHER_TURN[g]) if at == turn]
+             for turn in range(max(map(max, GATHER_TURN)) + 1)]
+    for turn in turns[:SLOT_TURN]:
         for g, i in turn:
             both(gather, g, lambda ga: ga.step(i))
 
@@ -421,26 +431,27 @@
         def _():
             fetch(h + 2)
 
-        for late, turn in enumerate(turns[7:]):
+        @pl.when((h < n_pairs) & (lax.rem(h, pairs) == pairs - 1))
+        def _():
+            pair_start(h // pairs)
+
+        for late, turn in enumerate(turns[SLOT_TURN:]):
             @pl.when(h == late)
             def _():
                 for g, i in turn:
                     both(gather, g, lambda ga: ga.step(i))
 
         for i in reversed(range(5)):
-            k = (h - i) // pairs - 1
-
-            @pl.when((h >= i + pairs) & (lax.rem(h + pairs * 5 - i, pairs) == 0) & (k < n_chunks))
+            since = h - STEP_SLOT[i]
+            k = since // pairs - 1
+
+            @pl.when((since >= pairs) & (lax.rem(since + pairs * 5, pairs) == 0) & (k < n_chunks))
             def _():
                 scatter_step(k, i)
 
-        @pl.when((h < n_pairs) & (lax.rem(h, pairs) == pairs - 1))
-        def _():
-            pair_start(h // pairs)
-
         return carry
 
-    lax.fori_loop(0, n_pairs + 5, slot, 0)
+    lax.fori_loop(0, n_pairs + STEP_SLOT[4] + 1, slot, 0)
 
     def drain_gather(k, carry):
         both(gather, k, lambda g: g.drain())
@@ -452,11 +463,15 @@
             copy.wait_send()
         return carry
 
-    lax.fori_loop(0, n_gather, drain_gather, 0)
-    lax.fori_loop(0, n_chunks, drain, 0)
-
-
-def attention(side, lens, q, ckv, krt, q_len, scale, chunk, gather_pairs):
+    def drain_all():
+        both(gather, 0, lambda g: g.drain())
+        lax.fori_loop(1, n_gather, drain_gather, 0)
+        lax.fori_loop(0, n_chunks, drain, 0)
+
+    return drain_all
+
+
+def step(side, lens, q, ckv, krt, w_uv, wo, hidden, q_len, scale, chunk, gather_pairs):
     batch, local_len, lat = ckv.shape
     rope = krt.shape[1]
     block = q.shape[1]
@@ -486,16 +501,42 @@
         dma((n, 2, 2 * SCATTER_MSGS)), dma((n, 2, 2 * SCATTER_MSGS)),
         dma((n, 2)), dma((n, 2)), dma((4,)), dma((4,)),
     ]
+    tokens, width = hidden.shape[1:]
+    rb = batch * tokens // (side * side)
+    mine = width // CORES
+    cols = mine // PARTS // 2
+    far = cols - cols // 256 * 128
+    out_scratch = [
+        pltpu.VMEM((side, side, rb, width), F32),
+        pltpu.VMEM(wo.shape, BF16),
+        pltpu.VMEM((rb // tokens, tokens, mine), BF16),
+        pltpu.VMEM((PARTS, 2, side, side, rb, cols), F32),
+        pltpu.VMEM((PARTS, 2, 2, side, rb, far), F32),
+        pltpu.VMEM((PARTS, 2, 2, side, rb, cols), F32),
+        pltpu.VMEM((PARTS, 2, 2, rb, far), F32),
+        pltpu.VMEM((PARTS, 2, 2, rb, cols), F32),
+        dma((PARTS, 2, SCATTER_MSGS)), dma((PARTS, 2, SCATTER_MSGS)),
+        dma((PARTS, 2, GATHER_MSGS)), dma((PARTS, 2, GATHER_MSGS)),
+        dma((PARTS, 2)), dma((PARTS, 2)), dma((2,)),
+    ]
+    vmem, hbm = pl.BlockSpec(memory_space=pltpu.VMEM), pl.BlockSpec(memory_space=pl.ANY)
     return pl.pallas_call(
-        functools.partial(attention_kernel, (side, chunk, gather_pairs, q_len, scale)),
-        out_shape=jax.ShapeDtypeStruct((batch, block, lat), BF16),
-        in_specs=[pl.BlockSpec(memory_space=pltpu.SMEM), pl.BlockSpec(memory_space=pltpu.VMEM),
-                  pl.BlockSpec(memory_space=pl.ANY), pl.BlockSpec(memory_space=pl.ANY)],
-        out_specs=pl.BlockSpec(memory_space=pltpu.VMEM),
-        scratch_shapes=scratch,
+        functools.partial(whole_kernel, (side, chunk, gather_pairs, q_len, scale), len(scratch)),
+        out_shape=jax.ShapeDtypeStruct((side, side, rb // tokens, tokens, width), BF16),
+        in_specs=[pl.BlockSpec(memory_space=pltpu.SMEM), vmem, hbm, hbm, vmem, hbm, hbm],
+        out_specs=vmem,
+        scratch_shapes=[pltpu.VMEM((batch, block, lat), BF16)] + scratch + out_scratch,
         compiler_params=pltpu.CompilerParams(collective_id=0, has_side_effects=True, vmem_limit_bytes=VMEM_BYTES),
-        name="attend_rings",
-    )(lens, q, ckv, krt)
+        name="latent_step",
+    )(lens, q, ckv, krt, w_uv, wo, hidden)
+
+
+def output_loads(place, wo_ref, hid_ref, wo_buf, hid_buf, lsem):
+    owned, _, mine = hid_buf.shape
+    spot = place.y * place.side + place.x
+    cols = pl.ds(pl.multiple_of(place.core * mine, 128), mine)
+    return (pltpu.make_async_copy(wo_ref, wo_buf, lsem.at[0]),
+            pltpu.make_async_copy(hid_ref.at[pl.ds(spot * owned, owned), :, cols], hid_buf, lsem.at[1]))
 
 
 def output_kernel(side, ol_ref, wuv_ref, wo_ref, hid_ref, out_ref, y_buf, wo_buf, hid_buf, pair_land, far1, near1, far2, near2,
@@ -505,23 +546,16 @@
     heads, _, value = wuv_ref.shape
     rb, width = y_buf.shape[2], y_buf.shape[3]
     mine = width // CORES
-    part, half = mine // 2, mine // 4
-    tiles = 4
-    tile = mine // tiles
-    n_rows = ol_ref.shape[0]
+    wide = mine // PARTS
+    part = wide // 2
+    half = part // 256 * 128
+    n_rows = ol_ref.shape[0] * ol_ref.shape[1]
     tokens = hid_ref.shape[1]
     owned = rb // tokens
 
-    wo_copy = pltpu.make_async_copy(wo_ref, wo_buf, lsem.at[0])
-    wo_copy.start()
-    col0 = pl.multiple_of(core * mine, 128)
-    spot = place.y * side + place.x
-    hid_copy = pltpu.make_async_copy(hid_ref.at[pl.ds(spot * owned, owned), :, pl.ds(col0, mine)], hid_buf, lsem.at[1])
-    hid_copy.start()
-    place.barrier()
-
+    wo_copy, hid_copy = output_loads(place, wo_ref, hid_ref, wo_buf, hid_buf, lsem)
     values = jnp.concatenate([wuv_ref[h] for h in range(heads)], axis=1)
-    ov = jnp.dot(ol_ref[...], values, preferred_element_type=F32)
+    ov = jnp.dot(ol_ref[...].reshape(-1, ol_ref.shape[-1]), values, preferred_element_type=F32)
     row_head = lax.rem(lax.broadcasted_iota(jnp.int32, ov.shape, 0) // tokens, heads)
     col_head = lax.broadcasted_iota(jnp.int32, ov.shape, 1) // value
     ov = jnp.where(row_head == col_head, ov, 0.0).astype(BF16)
@@ -532,116 +566,100 @@
     ov = jnp.dot(same.astype(F32).astype(BF16), ov, preferred_element_type=F32).astype(BF16)
     wo_copy.wait()
 
-    def columns(c, t):
-        return pl.ds(pl.multiple_of(c * mine + t * tile, 128), tile)
-
-    def compute(c, t):
-        y = jnp.dot(ov, wo_buf[:, columns(c, t)], preferred_element_type=F32)
-        y_buf[:, :, :, columns(c, t)] = y.reshape(side, side, rb, tile)
-
-    def pair_copy(t, arriving=False):
-        there = pair_land.at[t]
-        src = there if arriving else y_buf.at[:, :, :, columns(1 - core, t)]
-        return remote(src, there, psend.at[t], precv.at[t], place.sibling())
-
-    for t in range(tiles):
-        compute(1 - core, t)
-        pair_copy(t).start()
-    for t in range(tiles):
-        compute(core, t)
-        pair_copy(t, arriving=True).wait_recv()
-        y_buf[:, :, :, columns(core, t)] += pair_land[t]
-
-    def cols(plane, h, c):
-        lo, n = (0, part) if h is None else (h * half, half)
-        return pl.ds(pl.multiple_of(c * mine + plane * part + lo, 128), n)
-
-    def scatter(plane):
+    def span(h):
+        return {None: (0, part), 0: (0, half), 1: (half, part - half)}[h]
+
+    def cols(q, plane, h, c):
+        lo, n = span(h)
+        return pl.ds(pl.multiple_of(c * mine + q * wide + plane * part + lo, 128), n)
+
+    def compute(q, plane, c):
+        at = cols(q, plane, None, c)
+        y = jnp.dot(ov, wo_buf[:, at], preferred_element_type=F32)
+        y_buf[:, :, :, at] = y.reshape(side, side, rb, part)
+
+    def pair_copy(q, plane, arriving=False):
+        there = pair_land.at[q, plane]
+        src = there if arriving else y_buf.at[:, :, :, cols(q, plane, None, 1 - core)]
+        return remote(src, there, psend.at[q, plane], precv.at[q, plane], place.sibling())
+
+    def scatter(q, plane):
         def view(h, f, s):
             s = pl.ds(0, side) if s is None else s
             y, x = place.yx(plane, f, s)
-            return y_buf.at[y, x, :, cols(plane, h, core)]
+            return y_buf.at[y, x, :, cols(q, plane, h, core)]
 
         def landing(msg):
-            return {0: far1, 1: near1, 2: far2, 3: near2}[msg // 2].at[plane, msg % 2]
+            d = msg % 2
+            n = span(d)[1]
+            return {0: far1.at[q, plane, d, :, :, pl.ds(0, n)], 1: near1.at[q, plane, d],
+                    2: far2.at[q, plane, d, :, pl.ds(0, n)], 3: near2.at[q, plane, d]}[msg // 2]
 
         def merge(h, f, s, msg):
             y, x = place.yx(plane, f, pl.ds(0, side) if s is None else s)
-            y_buf[y, x, :, cols(plane, h, core)] += landing(msg)[...]
-
-        return Scatter(place, plane, view, landing, merge, lambda m: None, lambda m: ssend.at[plane, m],
-                       lambda m: srecv.at[plane, m])
-
-    scs = [scatter(plane) for plane in range(2)]
-    for sc in scs:
-        sc.start(0, 1)
-    for msg in (0, 1):
-        for sc in scs:
-            sc.take(msg)
-            sc.start(msg + 2)
-    for sc in scs:
-        sc.take(2)
-        sc.take(3)
-        sc.start(4, 5)
-    for msg in (4, 5):
-        for sc in scs:
-            sc.take(msg)
-            sc.start(msg + 2)
-    for sc in scs:
-        sc.take(6)
-        sc.take(7)
-    hid_copy.wait()
-    own = pl.ds(col0, mine)
-    total = y_buf[place.y, place.x, :, own] + hid_buf[...].astype(F32).reshape(rb, mine)
-    out_ref[place.y, place.x, :, own] = total.astype(BF16)
-
-    def gather(plane):
+            y_buf[y, x, :, cols(q, plane, h, core)] += landing(msg)[...]
+
+        return Scatter(place, plane, view, landing, merge, lambda m: None, lambda m: ssend.at[q, plane, m],
+                       lambda m: srecv.at[q, plane, m])
+
+    def gather(q, plane):
         def view(c, h, f, s):
             f = pl.ds(0, side) if f is None else f
             y, x = place.yx(plane, f, s)
-            return out_ref.at[y, x, :, cols(plane, h, c)]
+            return out_ref.at[y, x, :, :, cols(q, plane, h, c)]
 
         own = view(core, None, place.first[plane], place.second[plane])
-        return Gather(place, plane, view, own, lambda m: gsend.at[plane, m], lambda m: grecv.at[plane, m])
-
-    gs = [gather(plane) for plane in range(2)]
-    for i in range(1, 7):
-        for g in gs:
-            g.step(i)
-    for g in gs:
-        g.drain()
-    for sc in scs:
-        sc.drain()
-    for t in range(tiles):
-        pair_copy(t).wait_send()
-
-
-def output(side, ol, w_uv, wo, hidden):
-    batch, tokens, width = hidden.shape
-    rb = batch * tokens // (side * side)
-    mine = width // CORES
-    dma = pltpu.SemaphoreType.DMA
-    return pl.pallas_call(
-        functools.partial(output_kernel, side),
-        out_shape=jax.ShapeDtypeStruct((side, side, rb, width), BF16),
-        in_specs=[pl.BlockSpec(memory_space=pltpu.VMEM), pl.BlockSpec(memory_space=pltpu.VMEM),
-                  pl.BlockSpec(memory_space=pl.ANY), pl.BlockSpec(memory_space=pl.ANY)],
-        out_specs=pl.BlockSpec(memory_space=pltpu.VMEM),
-        scratch_shapes=[
-            pltpu.VMEM((side, side, rb, width), F32),
-            pltpu.VMEM(wo.shape, BF16),
-            pltpu.VMEM((rb // tokens, tokens, mine), BF16),
-            pltpu.VMEM((4, side, side, rb, mine // 4), F32),
-            pltpu.VMEM((2, 2, side, rb, mine // 4), F32),
-            pltpu.VMEM((2, 2, side, rb, mine // 2), F32),
-            pltpu.VMEM((2, 2, rb, mine // 4), F32),
-            pltpu.VMEM((2, 2, rb, mine // 2), F32),
-            dma((2, SCATTER_MSGS)), dma((2, SCATTER_MSGS)), dma((2, GATHER_MSGS)), dma((2, GATHER_MSGS)),
-            dma((4,)), dma((4,)), dma((2,)),
-        ],
-        compiler_params=pltpu.CompilerParams(collective_id=1, has_side_effects=True, vmem_limit_bytes=VMEM_BYTES),
-        name="project_rings",
-    )(ol, w_uv, wo, hidden)
+        return Gather(place, plane, view, own, lambda m: gsend.at[q, plane, m], lambda m: grecv.at[q, plane, m], True)
+
+    scs = [[scatter(q, plane) for plane in range(2)] for q in range(PARTS)]
+    gs = [[gather(q, plane) for plane in range(2)] for q in range(PARTS)]
+
+    for q in range(PARTS):
+        for plane in range(2):
+            compute(q, plane, 1 - core)
+            pair_copy(q, plane).start()
+    for q in range(PARTS):
+        for plane in range(2):
+            compute(q, plane, core)
+            pair_copy(q, plane, arriving=True).wait_recv()
+            y_buf[:, :, :, cols(q, plane, None, core)] += pair_land[q, plane]
+            scs[q][plane].start(0, 1)
+    hid_copy.wait()
+    for i in range(1, 5):
+        for q in range(PARTS):
+            for sc in scs[q]:
+                for msg in (2 * i - 2, 2 * i - 1):
+                    sc.take(msg)
+                    if i in (1, 3):
+                        sc.start(msg + 2)
+                if i == 2:
+                    sc.start(4, 5)
+            if i == 4:
+                own = pl.ds(pl.multiple_of(core * mine + q * wide, 128), wide)
+                total = y_buf[place.y, place.x, :, own].reshape(owned, tokens, wide)
+                total += hid_buf[:, :, q * wide:(q + 1) * wide].astype(F32)
+                out_ref[place.y, place.x, :, :, own] = total.astype(BF16)
+                for g in gs[q]:
+                    g.step(1)
+    for i in range(2, 5):
+        for q in range(PARTS):
+            for g in gs[q]:
+                g.step(i)
+    for q in range(PARTS):
+        for plane in range(2):
+            gs[q][plane].drain()
+            scs[q][plane].drain()
+            pair_copy(q, plane).wait_send()
+
+
+def whole_kernel(cfg, n_scratch, lens_ref, q_ref, ckv_ref, krt_ref, wuv_ref, wo_ref, hid_ref, out_ref, ol_buf, *scratch):
+    first, second = scratch[:n_scratch], scratch[n_scratch:]
+    wo_buf, hid_buf, lsem = second[1], second[2], second[-1]
+    for copy in output_loads(Place(cfg[0]), wo_ref, hid_ref, wo_buf, hid_buf, lsem):
+        copy.start()
+    drain = attention_kernel(cfg, lens_ref, q_ref, ckv_ref, krt_ref, ol_buf, *first)
+    output_kernel(cfg[0], ol_buf, wuv_ref, wo_ref, hid_ref, out_ref, *second)
+    drain()
 
 
 def solution(mesh):
@@ -656,14 +674,16 @@
         q_nope = jnp.einsum("cre,eil->cril", hidden, w_uq, preferred_element_type=F32).astype(BF16)
         q_rope = jnp.einsum("cre,eis->cris", hidden, w_qr, preferred_element_type=F32).astype(BF16)
         q_lat = jnp.einsum("bqhk,hkc->bqhc", q_nope, w_uk, preferred_element_type=F32).astype(BF16)
-        lat_pairs = q_lat.reshape(batch // 2, 2, tokens, heads, lat).transpose(0, 3, 2, 1, 4).reshape(batch // 2, block, 2 * lat)
-        rope_pairs = q_rope.reshape(batch // 2, 2, tokens, heads, rope).transpose(0, 3, 2, 1, 4).reshape(batch // 2, block, 2 * rope)
-        q = jnp.concatenate([lat_pairs, rope_pairs], axis=2)
-        ol = attention(side, cache_lens, q, c_kv, k_r.transpose(0, 2, 1), tokens, scale, batch // 8, batch // 8)
-        out = output(side, ol.reshape(batch * block, lat), w_uv, w_o.reshape(-1, width), hidden)
+        def paired(v):
+            v = v.reshape(batch // 2, 2, tokens, heads, -1).transpose(0, 3, 2, 1, 4)
+            return v.reshape(batch // 2, block, -1)
+
+        q = jnp.concatenate([paired(q_lat), paired(q_rope)], axis=2)
+        out = step(side, cache_lens, q, c_kv, k_r.transpose(0, 2, 1), w_uv, w_o.reshape(-1, width), hidden, tokens, scale,
+                   batch // 8, batch // 8)
         return out.reshape(batch, tokens, width)
 
-    specs_in = (P("batch", None, None), P("batch"), P("batch", "seq", None), P("batch", "seq", None),
-                P(None, "seq", None), P(None, "seq", None), P("seq", None, None), P("seq", None, None),
-                P("seq", None, None))
-    return jax.shard_map(local_step, mesh=mesh, in_specs=specs_in, out_specs=P("batch", None, None), check_vma=False)
+    rows, heads, middle = P("batch"), P("seq"), P(None, "seq")
+    cache = P("batch", "seq")
+    specs_in = (rows, rows, cache, cache, middle, middle, heads, heads, heads)
+    return jax.shard_map(local_step, mesh=mesh, in_specs=specs_in, out_specs=rows, check_vma=False)

time: 212 us -> 155 us (0.73)
  Pallas kernels: 199 us -> 143 us
    pallas_call x2 -> x1, Pallas kernels: 199 us -> 143 us  [step(): pl.pallas_call(functools.partial(whole_kernel, (side, chunk, gather_pairs...]
    reshape x6 -> x5, local copies, waits for them, and re-layouts: 4.71 us -> 0.66 us  [the longest x3 0.39 us: paired(): v = v.reshape(batch // 2, 2, tokens, heads, -1).transpose(0, 3, 2, 1, 4)]
    unnamed x4 -> x5, local copies, waits for them, and re-layouts: 0.01 us -> 3.37 us
where the time goes in v3:
time: 155 us; the launch traced here: 154 us
  Pallas kernels  143 us (92%)
  matrix products  6.48 us (4%)
  local copies, waits for them, and re-layouts  4.02 us (3%)
    pallas_call x1, Pallas kernels, step(): pl.pallas_call(functools.partial(whole_kernel, (side, chunk, gather_pairs...  143 us
    unnamed x5, local copies, waits for them, and re-layouts  3.37 us
    dot_general x1, matrix products, local_step(): jnp.einsum('cre,eis->cris', hidden, w_qr, preferred_element_type=F32)  3.31 us
    dot_general x1, matrix products, local_step(): jnp.einsum('bqhk,hkc->bqhc', q_nope, w_uk, preferred_element_type=F32)  3.17 us

profile of v3, /device:TPU:97, one launch (start us, length us, event | category | flops | bytes accessed | tf_op | source)
XLA Modules:
  0.0 154.4 jit_solution(9673314558426125755)
XLA Ops:
  0.0 0.0 copy-start
  0.0 0.0 copy-start.1
  0.0 3.3 %fusion.7 = bf16[32,4,2,64]{3,0,2,1:T(8,128)(2,1)S(1)} fusion(bf16[7168,2,64]{0,2,1:T(8,128)(2,1)} %param.14, bf16[32,4,7168,1]{2,1,0,3:T(4,128)(2,1)} %bitcast.32), kind=kOutput, calls=%fused_computation.8 | convolution fusion | flops 234897408 | bytes 3702784 | tf_op jit(solution)/shard_map/cre,eis->cris/dot_general | solution.py:675
  3.4 0.1 reshape.21
  3.5 0.0 copy-done
  3.5 0.0 copy-done.1
  3.5 3.2 %fusion.6 = bf16[32,4,2,512]{3,0,1,2:T(8,128)(2,1)S(1)} fusion(bf16[7168,2,128,1]{2,1,0,3:T(2,128)(2,1)} %bitcast.37, bf16[32,4,7168,1]{2,1,0,3:T(4,128)(2,1)S(1)} %bitcast.33, bf16[2,128,512]{2,1,0:T(8,128)(2,1)S(1)} %copy-done.1), kind=kOutput, calls=%fused_computation.7 | convolution fusion | flops 503480320 | bytes 6029312 | tf_op jit(solution)/shard_map/bqhk,hkc->bqhc/dot_general | solution.py:676
  6.7 0.1 reshape.18
  6.8 0.2 copy.37
  7.0 0.2 reshape.19
  7.2 0.7 pad_maximum_fusion.q_ref
  7.9 143.1 %latent_step.1 = bf16[4,4,2,4,7168]{4,3,2,1,0:T(4,128)(2,1)} custom-call(s32[32]{0:T(128)} %lens_ref.1, bf16[16,8,1152]{2,1,0:T(8,128)(2,1)} %pad_maximum_fusion.q_ref, bf16[32,1024,512]{2,1,0:T(8,128)(2,1)} %ckv_ref.1, bf16[32,64,1024]{2,1,0:T(8,128)(2,1)} %bitcast.30, bf16[2,512,128]{2,1,0:T(8,128)(2,1)} %wuv_ref.1, bf16[256,7168]{1,0:T(8,128)(2,1)} %bitcast.31, ...), custom_call_target="tpu_custom_call" | custom-call | tf_op jit(solution)/shard_map/latent_step/pallas_call | solution.py:523
  151.0 3.4 %copy.40 = bf16[32,4,7168]{2,1,0:T(4,128)(2,1)} copy(bf16[32,4,7168]{2,1,0:T(4,128)(2,1)} %bitcast.29) | data formatting | bytes 3670016
  (1 shorter events, 0.0 us)
Async XLA Ops:
  0.0 3.5 %copy-start = (bf16[32,4,7168]{2,1,0:T(4,128)(2,1)S(1)}, bf16[32,4,7168]{2,1,0:T(4,128)(2,1)}, u32[]{:S(2)}) copy-start(bf16[32,4,7168]{2,1,0:T(4,128)(2,1)} %hid_ref.1) | copy-start | bytes 5505028
  0.0 3.5 %copy-start.1 = (bf16[2,128,512]{2,1,0:T(8,128)(2,1)S(1)}, bf16[2,128,512]{2,1,0:T(8,128)(2,1)}, u32[]{:S(2)}) copy-start(bf16[2,128,512]{2,1,0:T(8,128)(2,1)} %param.15) | copy-start | bytes 786436
